TPU v7x, 32 devices: a whole 2x2x4 slice. The times are simulated.
32 devices in a mesh: seq: 8 (over y, x, core), head: 4 (over z).
Axes of the slice: x: 2, y: 2, z: 4, core: 2. Of those that a mesh axis runs over, the one named last changes fastest.
Arguments:
- key_rows: bfloat16 [2048, 2048], P('seq', 'head'), may hold values from -1 to 1, as said below
- values: bfloat16 [2048, 2048], P('seq', 'head'), may hold values from -6 to 6
- d_layer: bfloat16 [2048, 2048], P('seq', 'head'), may hold values from -6 to 6
- out_weight: bfloat16 [2048, 2048], P('head'), may hold values from -0.125 to 0.125
- saved_solutions: float32 [2048, 2048], P('seq', 'head'), may hold values from -0.625 to 0.625
- ridge_scale: float32 [16], P('head'), may hold values from 0.5 to 4
Outputs:
- grad_queries: float32 [2048, 2048], P('seq', 'head')
- grad_keys: float32 [2048, 2048], P('seq', 'head')
- grad_values: float32 [2048, 2048], P('seq', 'head')
Inputs may be any that keep to these rules, and one draw needn't show every extreme that they name: `key_rows`: within each head the 128 entries of a key have Euclidean norm 1 up to bfloat16 rounding.
All inputs are finite; a program needn't handle non-finite values.
Results may differ from a plain program's by a relative error of at most 0.0029.
Values may be sent and summed in bfloat16 or wider, within the bound.
A program may use at most 64 MiB of HBM per device.

v0:
```python
import functools
import jax
import jax.numpy as jnp
from jax import lax
from jax.experimental import pallas as pl
from jax.experimental.pallas import tpu as pltpu
from jax.sharding import PartitionSpec as P

DH = 128
ITERS = 8
EPSILON = 1e-06
BF = jnp.bfloat16
F32 = jnp.float32

def nn(left, right):
    return lax.dot_general(left, right, (((1,), (0,)), ((), ())), preferred_element_type=F32)


def nt(left, right):
    return lax.dot_general(left, right, (((1,), (1,)), ((), ())), preferred_element_type=F32)


def split(a):
    hi = a.astype(BF)
    return hi, (a - hi.astype(F32)).astype(BF)


def flip(a):
    return a.astype(F32).T.astype(BF)


def head(ref, h):
    return ref[:, h * DH : (h + 1) * DH]


def window_masked(scores):
    tok = scores.shape[1]
    key_ids = lax.broadcasted_iota(jnp.int32, (tok, tok), 0)
    tok_ids = lax.broadcasted_iota(jnp.int32, (tok, tok), 1)
    own = key_ids <= tok_ids
    return jnp.concatenate(
        [jnp.where(own, scores[:tok], 0.0), jnp.where(own, 0.0, scores[tok:])], axis=0
    )


def rows_sum(ref, h):
    total = None
    for slot in range(ref.shape[0]):
        part = ref[slot, h].astype(F32)
        total = part if total is None else total + part
    return total


def own_kernel(key, val, sol, sav, out, gk, gv):
    tok = key.shape[0]
    key_ids = lax.broadcasted_iota(jnp.int32, (tok, tok), 0)
    tok_ids = lax.broadcasted_iota(jnp.int32, (tok, tok), 1)
    later = tok_ids >= key_ids
    for h in range(key.shape[1] // DH):
        k, v, o = head(key, h), head(val, h), head(out, h)
        x_hi, x_lo = split(head(sav, h))
        y_hi, y_lo = split(-head(sol, h))
        a1 = nt(jnp.concatenate([k, k], axis=1), jnp.concatenate([x_hi, x_lo], axis=1))
        a2 = nt(jnp.concatenate([v, k], axis=1), jnp.concatenate([o, y_hi], axis=1)) + nt(k, y_lo)
        a1_hi, a1_lo = split(jnp.where(later, a1, 0.0))
        a2_hi, a2_lo = split(jnp.where(later, a2, 0.0))
        yo = jnp.concatenate([y_hi, o], axis=1)
        both = nn(a1_hi, yo) + nn(a1_lo, yo)
        g = both[:, :DH] + nn(a1_hi, y_lo) + nn(a2_hi, x_hi) + nn(a2_lo, x_hi) + nn(a2_hi, x_lo)
        gk[:, h * DH : (h + 1) * DH] = g
        gv[:, h * DH : (h + 1) * DH] = both[:, DH:]


def lead_kernel(key, val, sol, sav, out, pair, cross, gk_own, gv_own, gk, gv):
    tok = key.shape[0]
    key_ids = lax.broadcasted_iota(jnp.int32, (tok, tok), 0)
    tok_ids = lax.broadcasted_iota(jnp.int32, (tok, tok), 1)
    later = tok_ids < key_ids
    for h in range(key.shape[1] // DH):
        k, v, o, x, y = head(key, h), head(val, h), head(out, h), head(sav, h), -head(sol, h)
        vk = jnp.concatenate([v, k], axis=1)
        a1_hi, a1_lo = split(jnp.where(later, nt(k, x), 0.0))
        a2_hi, a2_lo = split(jnp.where(later, nt(vk, jnp.concatenate([o, y], axis=1)), 0.0))
        yo = jnp.concatenate([y, o], axis=1)
        c_hi, c_lo = split(rows_sum(cross, h))
        p_hi, p_lo = split(-rows_sum(pair, h))
        both = nn(a1_hi, yo) + nn(a1_lo, yo)
        both = both + nn(k, jnp.concatenate([p_hi, c_hi], axis=1)) + nn(k, jnp.concatenate([p_lo, c_lo], axis=1))
        g = both[:, :DH] + nn(a2_hi, x) + nn(a2_lo, x)
        g = g + nt(vk, jnp.concatenate([c_hi, p_hi], axis=1)) + nt(vk, jnp.concatenate([c_lo, p_lo], axis=1))
        at = slice(h * DH, (h + 1) * DH)
        gk[:, at] = gk_own[:, at] + g
        gv[:, at] = gv_own[:, at] + both[:, DH:]


def mega(span, n_seq, n_head, ridge, key_hbm, val_hbm, d_hbm, w_hbm, sav_hbm, sol, gk, gv,
         key, val, d_own, w, sav, sav_bf, out, sol_bf, gram, state, cross, pair,
         d_in, key_lag, val_lag, sav_lead, out_lead, sol_lead, gram_in, state_in, cross_in, pair_in,
         r_s, p_s, y_s, rr_s, k2_s, kt_s, g_s, local_sem, send_sem, recv_sem):
    s = lax.axis_index("seq")
    me = lax.axis_index("head")
    heads = gram.shape[0]
    tok = key.shape[0]
    w_copy = pltpu.make_async_copy(w_hbm, w, local_sem.at[0])
    x_copy = pltpu.make_async_copy(sav_hbm, sav, local_sem.at[1])
    inputs = [
        pltpu.make_async_copy(source, target, local_sem.at[2 + number])
        for number, (source, target) in enumerate([(key_hbm, key), (d_hbm, d_own), (val_hbm, val)])
    ]
    for copy in inputs:
        copy.start()
    w_copy.start()
    x_copy.start()

    offsets = [d for m in range(1, span + 1) for d in (m, -m)]

    def exists(d):
        return s + d < n_seq if d > 0 else s + d >= 0

    barrier = pltpu.get_barrier_semaphore()
    for j in range(1, n_head):
        pl.semaphore_signal(
            barrier, inc=1, device_id={"head": lax.rem(me + j, n_head)}, device_id_type=pl.DeviceIdType.MESH
        )
    for d in offsets:
        @pl.when(exists(d))
        def _():
            pl.semaphore_signal(barrier, inc=1, device_id={"seq": s + d}, device_id_type=pl.DeviceIdType.MESH)
    pl.semaphore_wait(
        barrier, n_head - 1 + jnp.minimum(s, span) + jnp.minimum(n_seq - 1 - s, span)
    )

    counter = [0]
    sends = []

    class Hop:
        def __init__(self, source, target, d):
            self.d = d
            self.copy = pltpu.make_async_remote_copy(
                src_ref=source,
                dst_ref=target,
                send_sem=send_sem.at[counter[0]],
                recv_sem=recv_sem.at[counter[0]],
                device_id={"seq": s + d},
                device_id_type=pl.DeviceIdType.MESH,
            )
            counter[0] += 1
            sends.append(self)

            @pl.when(jnp.logical_not(exists(-d)))
            def _():
                target[...] = jnp.zeros(target.shape, target.dtype)

        def start(self):
            pl.when(exists(self.d))(self.copy.start)
            return self

        def arrive(self):
            pl.when(exists(-self.d))(self.copy.wait_recv)

        def finish(self):
            pl.when(exists(self.d))(self.copy.wait_send)

    def mids(source, target, sign):
        return [Hop(source, target.at[m - 1], sign * m).start() for m in range(1, span)]

    for copy in inputs:
        copy.wait()
    key_hop = Hop(key, key_lag, span).start()
    d_copies = []
    for j in range(1, n_head):
        copy = pltpu.make_async_remote_copy(
            src_ref=d_own,
            dst_ref=d_in.at[j - 1],
            send_sem=send_sem.at[counter[0]],
            recv_sem=recv_sem.at[counter[0]],
            device_id={"head": lax.rem(me + j, n_head)},
            device_id_type=pl.DeviceIdType.MESH,
        )
        counter[0] += 1
        copy.start()
        d_copies.append(copy)
    val_hop = Hop(val, val_lag, span).start()

    for h in range(heads):
        k = head(key, h)
        both = nn(flip(k), jnp.concatenate([k, head(val, h)], axis=1)).astype(BF)
        gram[h] = both[:, :DH]
        state[h] = both[:, DH:]
    state_hops = mids(state, state_in, 1)
    gram_hops = mids(gram, gram_in, 1)
    x_copy.wait()
    sav_bf[...] = sav[...].astype(BF)
    sav_hop = Hop(sav_bf, sav_lead, -span).start()

    w_copy.wait()
    width = d_own.shape[1]
    acc = None
    for j in range(n_head):
        if j:
            d_copies[j - 1].wait_recv()
        piece = d_own[...] if j == 0 else d_in[j - 1]
        col = lax.rem(me + (n_head - j), n_head) * width
        part = nt(piece, w[:, pl.ds(pl.multiple_of(col, width), width)])
        acc = part if acc is None else acc + part
    out[...] = acc.astype(BF)
    out_hop = Hop(out, out_lead, -span).start()
    for h in range(heads):
        x_hi, x_lo = split(head(sav, h).T)
        o = head(out, h)
        cross[h] = (nn(x_hi, o) + nn(x_lo, o)).astype(BF)
    cross_hops = mids(cross, cross_in, -1)

    key_hop.arrive()
    for h in range(heads):
        k_cat = jnp.concatenate([head(key, h), head(key_lag, h)], axis=0)
        k2_s[h] = jnp.concatenate([k_cat, k_cat], axis=1)
        kt_s[h] = flip(k_cat)
    val_hop.arrive()
    for hop in state_hops + gram_hops:
        hop.arrive()
    for h in range(heads):
        o = head(out, h)
        v_cat = jnp.concatenate([head(val, h), head(val_lag, h)], axis=0)
        s_hi, s_lo = split(window_masked(nt(v_cat, o)))
        st_hi, st_lo = split(rows_sum(state_in, h))
        r = nn(kt_s[h], s_hi) + nn(kt_s[h], s_lo) + nt(st_hi, o) + nt(st_lo, o)
        g_hi, g_lo = split(rows_sum(gram_in, h))
        g_s[h] = jnp.concatenate([g_hi, g_hi, g_lo], axis=1)
        r_s[h] = r
        p_s[h] = r
        y_s[h] = jnp.zeros_like(r)
        rr_s[h] = jnp.sum(r * r, axis=0, keepdims=True)

    def step(_, carry):
        for h in range(heads):
            p = p_s[h]
            p_hi, p_lo = split(p)
            scores = nn(k2_s[h], jnp.concatenate([p_hi, p_lo], axis=0))
            masked = window_masked(scores).astype(BF)
            image = nn(kt_s[h], masked) + nn(g_s[h], jnp.concatenate([p_hi, p_lo, p_hi], axis=0))
            image = image + ridge[h] * p
            rr = rr_s[h]
            alpha = rr / (jnp.sum(p * image, axis=0, keepdims=True) + EPSILON)
            y_s[h] = y_s[h] + alpha * p
            r = r_s[h] - alpha * image
            r_s[h] = r
            nr = jnp.sum(r * r, axis=0, keepdims=True)
            p_s[h] = r + nr / (rr + EPSILON) * p
            rr_s[h] = nr
        return carry

    lax.fori_loop(0, ITERS, step, 0)
    for h in range(heads):
        y = y_s[h].T
        sol[:, h * DH : (h + 1) * DH] = y
        sol_bf[:, h * DH : (h + 1) * DH] = y.astype(BF)
    sol_hop = Hop(sol_bf, sol_lead, -span).start()
    for h in range(heads):
        y_hi, y_lo = split(head(sol, h))
        x_hi, x_lo = split(head(sav, h).T)
        pair[h] = (nn(x_hi, y_hi) + nn(x_lo, y_hi) + nn(x_hi, y_lo)).astype(BF)
    pair_hops = mids(pair, pair_in, -1)

    own_kernel(key, val, sol, sav, out, gk, gv)
    for hop in [sav_hop, out_hop] + cross_hops + [sol_hop] + pair_hops:
        hop.arrive()
    lead_kernel(key, val, sol_lead, sav_lead, out_lead, pair_in, cross_in, gk, gv, gk, gv)
    for copy in d_copies:
        copy.wait_send()
    for hop in sends:
        hop.finish()


def body(key_rows, values, d_layer, out_weight, saved_solutions, ridge_scale):
    tok, cols = key_rows.shape
    heads = cols // DH
    n_seq, n_head = lax.axis_size("seq"), lax.axis_size("head")
    span = n_seq // 4
    slots = max(span - 1, 1)
    copies = n_head - 1 + 5 + 4 * (span - 1)
    vmem = pl.BlockSpec(memory_space=pltpu.VMEM)
    smem = pl.BlockSpec(memory_space=pltpu.SMEM)
    hbm = pl.BlockSpec(memory_space=pltpu.HBM)
    flat = jax.ShapeDtypeStruct((tok, cols), F32)
    half = pltpu.VMEM((tok, cols), BF)
    mats = pltpu.VMEM((heads, DH, DH), BF)
    mats_in = pltpu.VMEM((slots, heads, DH, DH), BF)
    vec = pltpu.VMEM((heads, DH, tok), F32)
    return pl.pallas_call(
        functools.partial(mega, span, n_seq, n_head),
        name="layer",
        out_shape=[flat, flat, flat],
        in_specs=[smem, hbm, hbm, hbm, hbm, hbm],
        out_specs=[vmem, vmem, vmem],
        scratch_shapes=[
            half, half, pltpu.VMEM(d_layer.shape, BF),
            pltpu.VMEM(out_weight.shape, BF), pltpu.VMEM((tok, cols), F32), half, half, half,
            mats, mats, mats, mats,
            pltpu.VMEM((n_head - 1,) + d_layer.shape, BF), half, half, half, half, half,
            mats_in, mats_in, mats_in, mats_in,
            vec, vec, vec,
            pltpu.VMEM((heads, 1, tok), F32),
            pltpu.VMEM((heads, 2 * tok, 2 * DH), BF),
            pltpu.VMEM((heads, DH, 2 * tok), BF),
            pltpu.VMEM((heads, DH, 3 * DH), BF),
            pltpu.SemaphoreType.DMA((5,)),
            pltpu.SemaphoreType.DMA((copies,)),
            pltpu.SemaphoreType.DMA((copies,)),
        ],
        compiler_params=pltpu.CompilerParams(
            collective_id=0, has_side_effects=True, vmem_limit_bytes=67043328
        ),
    )(ridge_scale, key_rows, values, d_layer, out_weight, saved_solutions)


def solution(mesh):
    return jax.shard_map(
        body,
        mesh=mesh,
        in_specs=(
            P("seq", "head"),
            P("seq", "head"),
            P("seq", "head"),
            P("head", None),
            P("seq", "head"),
            P("head"),
        ),
        out_specs=(P("seq", "head"), P("seq", "head"), P("seq", "head")),
        check_vma=False,
    )
```

profile of v0, /device:TPU:11, one launch (start us, length us, event | category | flops | bytes accessed | tf_op | source)
XLA Modules:
  0.0 54.8 jit_solution(5219213870168799509)
XLA Ops:
  0.6 49.6 %layer.1 = (f32[256,512]{1,0:T(8,128)}, f32[256,512]{1,0:T(8,128)}, f32[256,512]{1,0:T(8,128)}) custom-call(f32[4]{0:T(128)} %ridge.1, bf16[256,512]{1,0:T(8,128)(2,1)} %key_hbm.1, bf16[256,512]{1,0:T(8,128)(2,1)} %val_hbm.1, bf16[256,512]{1,0:T(8,128)(2,1)} %d_hbm.1, bf16[512,2048]{1,0:T(8,128)(2,1)} %w_hbm.1, f32[256,512]{1,0:T(8,128)} %sav_hbm.1), custom_call_target="tpu_custom_call" | custom-call | tf_op jit(solution)/shard_map/layer/pallas_call | solution.py:290
  50.2 0.0 copy-start
  50.2 1.9 %copy.12 = f32[256,512]{1,0:T(8,128)} copy(f32[256,512]{1,0:T(8,128)} %get-tuple-element.6) | data formatting | bytes 1048576
  52.2 1.9 %copy.13 = f32[256,512]{1,0:T(8,128)} copy(f32[256,512]{1,0:T(8,128)} %get-tuple-element.7) | data formatting | bytes 1048576
  54.0 0.0 copy-done
  54.0 0.8 %copy.14 = f32[256,512]{1,0:T(8,128)} copy(f32[256,512]{1,0:T(8,128)S(1)} %copy-done) | data formatting | bytes 1048576
Async XLA Ops:
  50.2 3.8 %copy-start = (f32[256,512]{1,0:T(8,128)S(1)}, f32[256,512]{1,0:T(8,128)}, u32[]{:S(2)}) copy-start(f32[256,512]{1,0:T(8,128)} %get-tuple-element.8) | copy-start | bytes 1572868
where the time goes:
time: 55 us; the launch traced here: 54.8 us
  Pallas kernels  49.6 us (90%)
  local copies, waits for them, and re-layouts  4.59 us (8%)
  between operations  0.65 us (1%)
    pallas_call x1, Pallas kernels, body(): pl.pallas_call(functools.partial(mega, span, n_seq, n_head), name='layer'...  49.6 us
    unnamed x5, local copies, waits for them, and re-layouts  4.59 us

commit v1 on v0

v1 whole, which is shorter than its diff:
```python
import functools
import jax
import jax.numpy as jnp
from jax import lax
from jax.experimental import pallas as pl
from jax.experimental.pallas import tpu as pltpu
from jax.sharding import PartitionSpec as P

DH = 128
ITERS = 8
EPSILON = 1e-06
BF = jnp.bfloat16
F32 = jnp.float32
MESH = pl.DeviceIdType.MESH


def nn(left, right):
    return lax.dot_general(left, right, (((1,), (0,)), ((), ())), preferred_element_type=F32)


def nt(left, right):
    return lax.dot_general(left, right, (((1,), (1,)), ((), ())), preferred_element_type=F32)


def split(a):
    hi = a.astype(BF)
    return hi, (a - hi.astype(F32)).astype(BF)


def flip(a):
    return a.astype(F32).T.astype(BF)


def beside(*parts):
    return jnp.concatenate(parts, axis=1)


def above(*parts):
    return jnp.concatenate(parts, axis=0)


def own_mask(tok):
    key_ids = lax.broadcasted_iota(jnp.int32, (tok, tok), 0)
    tok_ids = lax.broadcasted_iota(jnp.int32, (tok, tok), 1)
    return key_ids <= tok_ids


def window_masked(scores):
    tok = scores.shape[1]
    own = own_mask(tok)
    return above(jnp.where(own, scores[:tok], 0.0), jnp.where(own, 0.0, scores[tok:]))


def slots_sum(ref, h):
    total = ref[0, h].astype(F32)
    for slot in range(1, ref.shape[0]):
        total = total + ref[slot, h].astype(F32)
    return total


def mega(span, n_seq, n_head, ridge_hbm, key_hbm, val_hbm, d_hbm, w_hbm, sav_hbm, sol, gk, gv,
         ridge, key, val, d_all, w, sav, out, key_lag, val_lag,
         gram, state, cross, sym, gram_in, state_in, cross_in, sym_in,
         gkl, gvl, gkl_bf, gvl_bf, gkl_in, gvl_in,
         k2_s, kt_s, a1_s, vs_s, xt_s, full_s, g_s, st_s, sym_s, r_s, p_s, y_s, rr_s,
         local_sem, dsend_sem, drecv_sem, send_sem, recv_sem):
    s = lax.axis_index("seq")
    me = lax.axis_index("head")
    heads = ridge.shape[0]
    tok = key.shape[0]
    half = tok // 2
    width = d_all.shape[2]
    mids_exist = span > 1
    rows = [slice(0, half), slice(half, tok)]
    d_copy_in = pltpu.make_async_copy(d_hbm, d_all.at[me], local_sem.at[0])
    key_copy = pltpu.make_async_copy(key_hbm, key, local_sem.at[1])
    val_copy = pltpu.make_async_copy(val_hbm, val, local_sem.at[2])
    w_copy = pltpu.make_async_copy(w_hbm, w, local_sem.at[3])
    x_copy = pltpu.make_async_copy(sav_hbm, sav, local_sem.at[4])
    ridge_copy = pltpu.make_async_copy(ridge_hbm, ridge, local_sem.at[5])
    for copy in (d_copy_in, key_copy, val_copy, x_copy, w_copy, ridge_copy):
        copy.start()

    def exists(d):
        return s + d < n_seq if d > 0 else s + d >= 0

    barrier = pltpu.get_barrier_semaphore()
    has_right, has_left = me + 1 < n_head, me > 0
    for there, step in ((has_right, 1), (has_left, -1)):
        @pl.when(there)
        def _():
            pl.semaphore_signal(barrier, inc=1, device_id={"head": me + step}, device_id_type=MESH)
    for d in [d for m in range(1, span + 1) for d in (m, -m)]:
        @pl.when(exists(d))
        def _():
            pl.semaphore_signal(barrier, inc=1, device_id={"seq": s + d}, device_id_type=MESH)
    pl.semaphore_wait(
        barrier,
        jnp.minimum(me, 1) + jnp.minimum(n_head - 1 - me, 1)
        + jnp.minimum(s, span) + jnp.minimum(n_seq - 1 - s, span),
    )

    counter = [0]
    sends = []

    class Hop:
        def __init__(self, source, target, d):
            self.d = d
            self.copy = pltpu.make_async_remote_copy(
                src_ref=source,
                dst_ref=target,
                send_sem=send_sem.at[counter[0]],
                recv_sem=recv_sem.at[counter[0]],
                device_id={"seq": s + d},
                device_id_type=MESH,
            )
            counter[0] += 1
            sends.append(self)

            @pl.when(jnp.logical_not(exists(-d)))
            def _():
                target[...] = jnp.zeros(target.shape, target.dtype)

        def start(self):
            pl.when(exists(self.d))(self.copy.start)
            return self

        def arrive(self):
            pl.when(exists(-self.d))(self.copy.wait_recv)

        def finish(self):
            pl.when(exists(self.d))(self.copy.wait_send)

    def mids(source, target, sign):
        return [Hop(source, target.at[m - 1], sign * m).start() for m in range(1, span)]

    def d_copy(origin, c, step):
        piece = d_all.at[origin, pl.ds(c * half, half)]
        place = origin * 2 + c
        return pltpu.make_async_remote_copy(
            src_ref=piece,
            dst_ref=piece,
            send_sem=dsend_sem.at[place + (0 if step > 0 else 2 * n_head)],
            recv_sem=drecv_sem.at[place],
            device_id={"head": me + step},
            device_id_type=MESH,
        )

    def d_start(c):
        pl.when(has_right)(lambda: d_copy(me, c, 1).start())
        pl.when(has_left)(lambda: d_copy(me, c, -1).start())

    def d_relay(c):
        for k in range(1, n_head - 1):
            @pl.when(jnp.logical_and(me - k >= 0, has_right))
            def _():
                copy = d_copy(me - k, c, 1)
                copy.wait_recv()
                copy.start()

            @pl.when(jnp.logical_and(me + k < n_head, has_left))
            def _():
                copy = d_copy(me + k, c, -1)
                copy.wait_recv()
                copy.start()

    at_end = jnp.logical_or(me == 0, me == n_head - 1)

    def project(c):
        acc = None
        for i in range(n_head):
            origin = jnp.where(me == 0, i, n_head - 1 - i)
            if i:
                pl.when(at_end)(lambda: d_copy(origin, c, 1).wait_recv())
            col = pl.multiple_of(origin * width, width)
            part = nt(d_all[origin, rows[c]], w[:, pl.ds(col, width)])
            acc = part if acc is None else acc + part
        out[rows[c]] = acc.astype(BF)

    def cols(h):
        return slice(h * DH, (h + 1) * DH)

    d_copy_in.wait()
    d_start(0)
    key_copy.wait()
    key_hop = Hop(key, key_lag, span).start()
    val_copy.wait()
    val_hop = Hop(val, val_lag, span).start()
    for h in range(heads):
        total = None
        for c in range(2):
            k = key[rows[c], cols(h)]
            kt = flip(k)
            kt_s[c, h, :, :half] = kt
            k2_s[c, h, :half] = beside(k, k)
            both = nn(kt, beside(k, val[rows[c], cols(h)]))
            if c == 0:
                full_s[1, h] = both
            total = both if total is None else total + both
        gram[h] = total[:, :DH].astype(BF)
        state[h] = total[:, DH:].astype(BF)
    state_hops = mids(state, state_in, 1)
    gram_hops = mids(gram, gram_in, 1)
    d_relay(0)
    d_start(1)
    x_copy.wait()
    for h in range(heads):
        for c in range(2):
            x_hi, x_lo = split(sav[rows[c], cols(h)].T)
            xt_s[c, h] = beside(x_hi, x_lo)
    d_relay(1)
    w_copy.wait()
    ridge_copy.wait()
    project(0)

    key_hop.arrive()
    for h in range(heads):
        for c in range(2):
            k = key_lag[rows[c], cols(h)]
            kt_s[c, h, :, half:] = flip(k)
            k2_s[c, h, half:] = beside(k, k)
            x2 = beside(*split(sav[rows[c], cols(h)]))
            a1 = window_masked(nt(k2_s[c, h], x2))
            a1_s[c, h] = beside(*split(a1))
    val_hop.arrive()
    for h in range(heads):
        lag = rows[1]
        full_s[0, h] = nn(kt_s[1, h, :, half:], beside(key_lag[lag, cols(h)], val_lag[lag, cols(h)]))
    for hop in state_hops + gram_hops:
        hop.arrive()
    for h in range(heads):
        for c in range(2):
            g, st = full_s[c, h, :, :DH], full_s[c, h, :, DH:]
            if mids_exist:
                g = g + slots_sum(gram_in, h)
                st = st + slots_sum(state_in, h)
            g_hi, g_lo = split(g)
            g_s[c, h] = beside(g_hi, g_hi, g_lo)
            st_s[c, h] = beside(*split(st))

    def begin(c):
        for h in range(heads):
            o = out[rows[c], cols(h)]
            v = above(val[rows[c], cols(h)], val_lag[rows[c], cols(h)])
            scores = window_masked(nt(v, o))
            vs_s[c, h] = scores
            s_hi, s_lo = split(scores)
            r = nn(kt_s[c, h], s_hi) + nn(kt_s[c, h], s_lo) + nt(st_s[c, h], beside(o, o))
            r_s[h] = r
            p_s[h] = r
            y_s[h] = jnp.zeros_like(r)
            rr_s[h] = jnp.sum(r * r, axis=0, keepdims=True)

    def cross_part(c):
        for h in range(heads):
            o = out[rows[c], cols(h)]
            o2 = above(o, o)
            both = nn(a1_s[c, h], o2)
            cross_c = nn(xt_s[c, h], o2)
            c_hi, c_lo = split(cross_c)
            if c == 0:
                gv[rows[0], cols(h)] = both[:half]
                gvl[rows[0], cols(h)] = both[half:]
                sym_s[h] = cross_c
                k2, v = k2_s[1, h, half:], val_lag[rows[1], cols(h)]
                gvl[rows[1], cols(h)] = nn(k2, above(c_hi, c_lo))
                gkl[rows[1], cols(h)] = nt(beside(v, v), beside(c_hi, c_lo))
                gvl_bf[rows[0], cols(h)] = both[half:].astype(BF)
            else:
                gv[rows[1], cols(h)] = both[:half]
                gvl_bf[rows[1], cols(h)] = (gvl[rows[1], cols(h)] + both[half:]).astype(BF)
                cross[h] = (sym_s[h] + cross_c).astype(BF)
                k2, v = k2_s[0, h, :half], val[rows[0], cols(h)]
                gv[rows[0], cols(h)] = gv[rows[0], cols(h)] + nn(k2, above(c_hi, c_lo))
                gk[rows[0], cols(h)] = gk[rows[0], cols(h)] + nt(beside(v, v), beside(c_hi, c_lo))

    def solve(c):
        def step(_, carry):
            for h in range(heads):
                p = p_s[h]
                p_hi, p_lo = split(p)
                scores = nn(k2_s[c, h], above(p_hi, p_lo))
                masked = window_masked(scores).astype(BF)
                image = nn(kt_s[c, h], masked) + nn(g_s[c, h], above(p_hi, p_lo, p_hi))
                image = image + ridge[h] * p
                rr = rr_s[h]
                alpha = rr / (jnp.sum(p * image, axis=0, keepdims=True) + EPSILON)
                y_s[h] = y_s[h] + alpha * p
                r = r_s[h] - alpha * image
                r_s[h] = r
                nr = jnp.sum(r * r, axis=0, keepdims=True)
                p_s[h] = r + nr / (rr + EPSILON) * p
                rr_s[h] = nr
            return carry

        lax.fori_loop(0, ITERS, step, 0)

    def key_part(c, h, which):
        y_hi, y_lo = split(y_s[h])
        part = slice(0, half) if which == 0 else slice(half, tok)
        scores = nn(k2_s[c, h, part], above(y_hi, y_lo))
        own = own_mask(half)
        scores = jnp.where(own, scores, 0.0) if which == 0 else jnp.where(own, 0.0, scores)
        a2_hi, a2_lo = split(vs_s[c, h, part] - scores)
        x_hi, x_lo = split(sav[rows[c], cols(h)])
        a1 = a1_s[c, h, part]
        g = nn(beside(a2_hi, a2_lo), above(x_hi, x_hi)) + nn(a2_hi, x_lo)
        return g - nt(a1, beside(y_hi, y_hi)) - nt(a1[:, :half], y_lo)

    def sym_part(c, h):
        y_hi, y_lo = split(-y_s[h])
        pair = nt(xt_s[c, h], beside(y_hi, y_hi)) + nt(xt_s[c, h, :, :half], y_lo)
        return pair + pair.T

    begin(0)
    cross_part(0)
    gva_hop = Hop(gvl_bf.at[pl.ds(0, half)], gvl_in.at[pl.ds(0, half)], -span).start()
    solve(0)
    for h in range(heads):
        gkl_bf[rows[0], cols(h)] = key_part(0, h, 1).astype(BF)
    gka_hop = Hop(gkl_bf.at[pl.ds(0, half)], gkl_in.at[pl.ds(0, half)], -span).start()
    for h in range(heads):
        gk[rows[0], cols(h)] = key_part(0, h, 0)
        sy = sym_part(0, h)
        sym_s[heads + h] = sy
        gkl[rows[1], cols(h)] = gkl[rows[1], cols(h)] + nn(k2_s[1, h, half:], above(*split(sy)))
        sol[rows[0], cols(h)] = y_s[h].T
    project(1)
    begin(1)
    cross_part(1)
    gvb_hop = Hop(gvl_bf.at[pl.ds(half, half)], gvl_in.at[pl.ds(half, half)], -span).start()
    cross_hops = mids(cross, cross_in, -1)
    solve(1)
    for h in range(heads):
        gkl_bf[rows[1], cols(h)] = (gkl[rows[1], cols(h)] + key_part(1, h, 1)).astype(BF)
    gkb_hop = Hop(gkl_bf.at[pl.ds(half, half)], gkl_in.at[pl.ds(half, half)], -span).start()
    for h in range(heads):
        sy = sym_part(1, h)
        sym[h] = (sym_s[heads + h] + sy).astype(BF)
        sym_s[h] = sy
    sym_hops = mids(sym, sym_in, -1)
    for h in range(heads):
        gk[rows[1], cols(h)] = key_part(1, h, 0)
        gk[rows[0], cols(h)] = gk[rows[0], cols(h)] + nn(k2_s[0, h, :half], above(*split(sym_s[h])))
        sol[rows[1], cols(h)] = y_s[h].T
    for hop in [gva_hop, gvb_hop] + cross_hops:
        hop.arrive()
    for h in range(heads):
        v_add = gvl_in[:, cols(h)].astype(F32)
        if mids_exist:
            k, v = key[:, cols(h)], val[:, cols(h)]
            c_hi, c_lo = split(slots_sum(cross_in, h))
            v_add = v_add + nn(beside(k, k), above(c_hi, c_lo))
            gk[:, cols(h)] = gk[:, cols(h)] + nt(beside(v, v), beside(c_hi, c_lo))
        gv[:, cols(h)] = gv[:, cols(h)] + v_add
    for hop in [gka_hop, gkb_hop] + sym_hops:
        hop.arrive()
    for h in range(heads):
        k_add = gkl_in[:, cols(h)].astype(F32)
        if mids_exist:
            k = key[:, cols(h)]
            k_add = k_add + nn(beside(k, k), above(*split(slots_sum(sym_in, h))))
        gk[:, cols(h)] = gk[:, cols(h)] + k_add
    for j in range(n_head):
        for c in range(2):
            pl.when(jnp.logical_and(has_right, j <= me))(lambda: d_copy(j, c, 1).wait_send())
            pl.when(jnp.logical_and(has_left, j >= me))(lambda: d_copy(j, c, -1).wait_send())
    for hop in sends:
        hop.finish()


def store(sol, gk, gv, sol_hbm, gk_hbm, gv_hbm, sem):
    copies = [
        pltpu.make_async_copy(source, target, sem.at[i])
        for i, (source, target) in enumerate([(sol, sol_hbm), (gk, gk_hbm), (gv, gv_hbm)])
    ]
    for copy in copies:
        copy.start()
    for copy in copies:
        copy.wait()


def body(key_rows, values, d_layer, out_weight, saved_solutions, ridge_scale):
    tok, cols = key_rows.shape
    heads = cols // DH
    half = tok // 2
    n_seq, n_head = lax.axis_size("seq"), lax.axis_size("head")
    span = n_seq // 4
    slots = max(span - 1, 1)
    copies = 6 + 4 * (span - 1)
    vmem = pl.BlockSpec(memory_space=pltpu.VMEM)
    hbm = pl.BlockSpec(memory_space=pltpu.HBM)
    flat = jax.ShapeDtypeStruct((tok, cols), F32)
    kept = pltpu.VMEM((tok, cols), F32)
    rows_bf = pltpu.VMEM((tok, cols), BF)
    rows_f = pltpu.VMEM((tok, cols), F32)
    mats = pltpu.VMEM((heads, DH, DH), BF)
    mats_in = pltpu.VMEM((slots, heads, DH, DH), BF)
    vec = pltpu.VMEM((heads, DH, half), F32)
    results = pl.pallas_call(
        functools.partial(mega, span, n_seq, n_head),
        name="layer",
        out_shape=[kept, kept, kept],
        in_specs=[hbm] * 6,
        out_specs=[vmem, vmem, vmem],
        scratch_shapes=[
            pltpu.SMEM((heads,), F32), rows_bf, rows_bf, pltpu.VMEM((n_head,) + d_layer.shape, BF),
            pltpu.VMEM(out_weight.shape, BF), rows_f, rows_bf, rows_bf, rows_bf,
            mats, mats, mats, mats, mats_in, mats_in, mats_in, mats_in,
            rows_f, rows_f, rows_bf, rows_bf, rows_bf, rows_bf,
            pltpu.VMEM((2, heads, tok, 2 * DH), BF),
            pltpu.VMEM((2, heads, DH, tok), BF),
            pltpu.VMEM((2, heads, tok, tok), BF),
            pltpu.VMEM((2, heads, tok, half), F32),
            pltpu.VMEM((2, heads, DH, tok), BF),
            pltpu.VMEM((2, heads, DH, 2 * DH), F32),
            pltpu.VMEM((2, heads, DH, 3 * DH), BF),
            pltpu.VMEM((2, heads, DH, 2 * DH), BF),
            pltpu.VMEM((2 * heads, DH, DH), F32),
            vec, vec, vec,
            pltpu.VMEM((heads, 1, half), F32),
            pltpu.SemaphoreType.DMA((6,)),
            pltpu.SemaphoreType.DMA((4 * n_head,)),
            pltpu.SemaphoreType.DMA((2 * n_head,)),
            pltpu.SemaphoreType.DMA((copies,)),
            pltpu.SemaphoreType.DMA((copies,)),
        ],
        compiler_params=pltpu.CompilerParams(
            collective_id=0, has_side_effects=True, vmem_limit_bytes=48 * 1024 * 1024
        ),
    )(*(
        pltpu.with_memory_space_constraint(array, pltpu.HBM)
        for array in (ridge_scale, key_rows, values, d_layer, out_weight, saved_solutions)
    ))
    return pl.pallas_call(
        store,
        name="store",
        out_shape=[flat, flat, flat],
        in_specs=[vmem, vmem, vmem],
        out_specs=[hbm, hbm, hbm],
        scratch_shapes=[pltpu.SemaphoreType.DMA((3,))],
        compiler_params=pltpu.CompilerParams(vmem_limit_bytes=8 * 1024 * 1024),
    )(*(pltpu.with_memory_space_constraint(result, pltpu.VMEM) for result in results))


def solution(mesh):
    return jax.shard_map(
        body,
        mesh=mesh,
        in_specs=(
            P("seq", "head"),
            P("seq", "head"),
            P("seq", "head"),
            P("head", None),
            P("seq", "head"),
            P("head"),
        ),
        out_specs=(P("seq", "head"), P("seq", "head"), P("seq", "head")),
        check_vma=False,
    )
```

time: 55 us -> 51.5 us (0.936)
  local copies, waits for them, and re-layouts: 4.59 us -> 0 us
  Pallas kernels: 49.6 us -> 50.7 us
    unnamed x5 -> x0, local copies, waits for them, and re-layouts: 4.59 us -> none
    pallas_call x0 -> x1, Pallas kernels: none -> 1.17 us  [body(): pl.pallas_call(store, name='store', out_shape=[flat, flat, flat], in_spec...]
where the time goes in v1:
time: 51.5 us; the launch traced here: 51.3 us
  Pallas kernels  50.7 us (98%)
  between operations  0.64 us (1%)
    pallas_call x1, Pallas kernels, body(): pl.pallas_call(functools.partial(mega, span, n_seq, n_head), name='layer'...  49.5 us
    pallas_call x1, Pallas kernels, body(): pl.pallas_call(store, name='store', out_shape=[flat, flat, flat], in_spec...  1.17 us

profile of v1, /device:TPU:11, one launch (start us, length us, event | category | flops | bytes accessed | tf_op | source)
XLA Modules:
  0.0 51.3 jit_solution(12765786767655000037)
XLA Ops:
  0.6 49.5 %layer.1 = (f32[256,512]{1,0:T(8,128)S(1)}, f32[256,512]{1,0:T(8,128)S(1)}, f32[256,512]{1,0:T(8,128)S(1)}) custom-call(f32[4]{0:T(128)} %ridge_hbm.1, bf16[256,512]{1,0:T(8,128)(2,1)} %key_hbm.1, bf16[256,512]{1,0:T(8,128)(2,1)} %val_hbm.1, bf16[256,512]{1,0:T(8,128)(2,1)} %d_hbm.1, bf16[512,2048]{1,0:T(8,128)(2,1)} %w_hbm.1, f32[256,512]{1,0:T(8,128)} %sav_hbm.1), custom_call_target="tpu_custom_call" | custom-call | tf_op jit(solution)/shard_map/layer/pallas_call | solution.py:400
  50.1 1.2 %store.1 = (f32[256,512]{1,0:T(8,128)}, f32[256,512]{1,0:T(8,128)}, f32[256,512]{1,0:T(8,128)}) custom-call(f32[256,512]{1,0:T(8,128)S(1)} %get-tuple-element.6.sol, f32[256,512]{1,0:T(8,128)S(1)} %get-tuple-element.7.gk, f32[256,512]{1,0:T(8,128)S(1)} %get-tuple-element.8.gv), custom_call_target="tpu_custom_call" | custom-call | tf_op jit(solution)/shard_map/store/pallas_call | solution.py:435

commit v2 on v1

v2 whole, which is shorter than its diff:
```python
import functools
import jax
import jax.numpy as jnp
from jax import lax
from jax.experimental import pallas as pl
from jax.experimental.pallas import tpu as pltpu
from jax.sharding import PartitionSpec as P

DH = 128
ITERS = 8
EPSILON = 1e-06
BF = jnp.bfloat16
F32 = jnp.float32
MESH = pl.DeviceIdType.MESH


def nn(left, right):
    return lax.dot_general(left, right, (((1,), (0,)), ((), ())), preferred_element_type=F32)


def nt(left, right):
    return lax.dot_general(left, right, (((1,), (1,)), ((), ())), preferred_element_type=F32)


def split(a):
    hi = a.astype(BF)
    return hi, (a - hi.astype(F32)).astype(BF)


def flip(a):
    return a.astype(F32).T.astype(BF)


def beside(*parts):
    return jnp.concatenate(parts, axis=1)


def above(*parts):
    return jnp.concatenate(parts, axis=0)


def own_mask(tok):
    key_ids = lax.broadcasted_iota(jnp.int32, (tok, tok), 0)
    tok_ids = lax.broadcasted_iota(jnp.int32, (tok, tok), 1)
    return key_ids <= tok_ids


def window_masked(scores):
    tok = scores.shape[1]
    own = own_mask(tok)
    return above(jnp.where(own, scores[:tok], 0.0), jnp.where(own, 0.0, scores[tok:]))


def slots_sum(ref, h):
    total = ref[0, h].astype(F32)
    for slot in range(1, ref.shape[0]):
        total = total + ref[slot, h].astype(F32)
    return total


def mega(span, n_seq, n_head, ridge_hbm, key_hbm, val_hbm, d_hbm, w_hbm, sav_hbm, gq, gk, gv,
         ridge, key, val, d_all, w, sav, key_lag, val_lag, o_s,
         mid, mid_lag, mid_in, cross, sym, cross_in, sym_in,
         gkl_bf, gvl_bf, gkl_in, gvl_in, gkl_s, gvl_s, gk_more, gv_more, cross_a, sym_a,
         k2_s, kt_s, vc_s, xs_s, xt_s, a1_s, vs_s, full_s, g_s, st_s, r_s, p_s, ya_s, yb_s, rr_s,
         local_sem, dsend_sem, drecv_sem, send_sem, recv_sem):
    s = lax.axis_index("seq")
    me = lax.axis_index("head")
    heads = ridge.shape[0]
    tok = key.shape[0]
    half = tok // 2
    width = d_all.shape[2]
    rows = [slice(0, half), slice(half, tok)]
    y_s = [ya_s, yb_s]
    d_copy_in = pltpu.make_async_copy(d_hbm, d_all.at[me], local_sem.at[0])
    key_copy = pltpu.make_async_copy(key_hbm, key, local_sem.at[1])
    val_copy = pltpu.make_async_copy(val_hbm, val, local_sem.at[2])
    w_copy = pltpu.make_async_copy(w_hbm, w, local_sem.at[3])
    x_copy = pltpu.make_async_copy(sav_hbm, sav, local_sem.at[4])
    ridge_copy = pltpu.make_async_copy(ridge_hbm, ridge, local_sem.at[5])
    for copy in (d_copy_in, key_copy, val_copy, x_copy, w_copy, ridge_copy):
        copy.start()

    def exists(d):
        return s + d < n_seq if d > 0 else s + d >= 0

    barrier = pltpu.get_barrier_semaphore()
    has_right, has_left = me + 1 < n_head, me > 0
    for there, step in ((has_right, 1), (has_left, -1)):
        @pl.when(there)
        def _():
            pl.semaphore_signal(barrier, inc=1, device_id={"head": me + step}, device_id_type=MESH)
    for d in [d for m in range(1, span + 1) for d in (m, -m)]:
        @pl.when(exists(d))
        def _():
            pl.semaphore_signal(barrier, inc=1, device_id={"seq": s + d}, device_id_type=MESH)
    pl.semaphore_wait(
        barrier,
        jnp.minimum(me, 1) + jnp.minimum(n_head - 1 - me, 1)
        + jnp.minimum(s, span) + jnp.minimum(n_seq - 1 - s, span),
    )

    counter = [0]
    hops = []

    class Hop:
        def __init__(self, source, target, d, sender=None, receiver=None):
            self.sender = exists(d) if sender is None else sender
            self.receiver = exists(-d) if receiver is None else receiver
            self.copy = pltpu.make_async_remote_copy(
                src_ref=source,
                dst_ref=target,
                send_sem=send_sem.at[counter[0]],
                recv_sem=recv_sem.at[counter[0]],
                device_id={"seq": s + d},
                device_id_type=MESH,
            )
            counter[0] += 1
            hops.append(self)
            if receiver is None:
                @pl.when(jnp.logical_not(self.receiver))
                def _():
                    target[...] = jnp.zeros(target.shape, target.dtype)

        def start(self):
            pl.when(self.sender)(self.copy.start)
            return self

        def arrive(self):
            pl.when(self.receiver)(self.copy.wait_recv)

        def finish(self):
            pl.when(self.sender)(self.copy.wait_send)

    def mids(source, target, sign):
        return [Hop(source, target.at[m - 1], sign * m).start() for m in range(1, span)]

    def d_copy(origin, c, step):
        piece = d_all.at[origin, pl.ds(c * half, half)]
        place = origin * 2 + c
        return pltpu.make_async_remote_copy(
            src_ref=piece,
            dst_ref=piece,
            send_sem=dsend_sem.at[place + (0 if step > 0 else 2 * n_head)],
            recv_sem=drecv_sem.at[place],
            device_id={"head": me + step},
            device_id_type=MESH,
        )

    def d_start(c):
        pl.when(has_right)(lambda: d_copy(me, c, 1).start())
        pl.when(has_left)(lambda: d_copy(me, c, -1).start())

    def d_relay(k, c):
        @pl.when(jnp.logical_and(me - k >= 0, has_right))
        def _():
            copy = d_copy(me - k, c, 1)
            copy.wait_recv()
            copy.start()

        @pl.when(jnp.logical_and(me + k < n_head, has_left))
        def _():
            copy = d_copy(me + k, c, -1)
            copy.wait_recv()
            copy.start()

    at_end = jnp.logical_or(me == 0, me == n_head - 1)

    def project(c):
        acc = None
        for i in range(n_head):
            origin = jnp.where(me == 0, i, n_head - 1 - i)
            if i:
                pl.when(at_end)(lambda: d_copy(origin, c, 1).wait_recv())
            col = pl.multiple_of(origin * width, width)
            part = nt(d_all[origin, rows[c]], w[:, pl.ds(col, width)])
            acc = part if acc is None else acc + part
        for h in range(heads):
            o_s[h, rows[c]] = acc[:, h * DH : (h + 1) * DH].astype(BF)

    def cols(h):
        return slice(h * DH, (h + 1) * DH)

    d_copy_in.wait()
    d_start(0)
    d_start(1)
    key_copy.wait()
    key_hop = Hop(key, key_lag, span).start()
    val_copy.wait()
    val_hop = Hop(val, val_lag, span).start()
    for h in range(heads):
        total = None
        for c in range(2):
            k, v = key[rows[c], cols(h)], val[rows[c], cols(h)]
            kt = flip(k)
            kt_s[c, h, :, :half] = kt
            k2_s[c, h, :half] = beside(k, k)
            vc_s[c, h, :half] = v
            both = nn(kt, beside(k, v))
            if c == 0:
                full_s[1, h] = both
            total = both if total is None else total + both
        mid[h] = total.astype(BF)
    paired = span == 2
    if paired:
        odd = lax.rem(s, 2) == 1
        even = jnp.logical_not(odd)
        mid_hops = [Hop(mid, mid_in.at[0], 1, even, odd).start()]
    else:
        mid_hops = mids(mid, mid_in, 1)
    x_copy.wait()
    for h in range(heads):
        xs_s[h] = beside(*split(sav[:, cols(h)]))
        for c in range(2):
            xt_s[c, h] = beside(*split(sav[rows[c], cols(h)].T))
    for k in range(1, n_head - 1):
        for c in range(2):
            d_relay(k, c)
    w_copy.wait()
    ridge_copy.wait()
    key_hop.arrive()
    for h in range(heads):
        for c in range(2):
            k = key_lag[rows[c], cols(h)]
            kt_s[c, h, :, half:] = flip(k)
            k2_s[c, h, half:] = beside(k, k)
    val_hop.arrive()
    for h in range(heads):
        for c in range(2):
            vc_s[c, h, half:] = val_lag[rows[c], cols(h)]
        late = nn(kt_s[1, h, :, half:], beside(k2_s[1, h, half:, :DH], vc_s[1, h, half:]))
        full_s[0, h] = late
        if paired:
            early = nn(kt_s[0, h, :, half:], beside(k2_s[0, h, half:, :DH], vc_s[0, h, half:]))
            mid_lag[h] = (early + late).astype(BF)
    if paired:
        mid_hops.append(Hop(mid_lag, mid_in.at[0], -1, odd, even).start())
    project(0)
    for hop in mid_hops:
        hop.arrive()
    for h in range(heads):
        for c in range(2):
            total = full_s[c, h]
            if span > 1:
                total = total + slots_sum(mid_in, h)
            g_hi, g_lo = split(total[:, :DH])
            g_s[c, h] = beside(g_hi, g_hi)
            st_s[c, h] = beside(*split(total[:, DH:]))

    def begin(c):
        for h in range(heads):
            o = o_s[h, rows[c]]
            scores = window_masked(nt(vc_s[c, h], o))
            vs_s[c, h] = scores
            s_hi, s_lo = split(scores)
            r = nn(kt_s[c, h], s_hi) + nn(kt_s[c, h], s_lo) + nt(st_s[c, h], beside(o, o))
            r_s[h] = r
            p_s[h] = r
            y_s[c][h] = jnp.zeros_like(r)
            rr_s[h] = jnp.sum(r * r, axis=0, keepdims=True)

    def lag_scores(c, h):
        a1_s[c, h] = beside(*split(window_masked(nt(k2_s[c, h], xs_s[h, rows[c]]))))

    def cross_part(c, h):
        o = o_s[h, rows[c]]
        o2 = above(o, o)
        both = nn(a1_s[c, h], o2)
        cross_c = nn(xt_s[c, h], o2)
        c_hi, c_lo = split(cross_c)
        if c == 0:
            k2, v = k2_s[1, h, half:], vc_s[1, h, half:]
            gv[h, rows[0]] = both[:half]
            gvl_bf[h, rows[0]] = both[half:].astype(BF)
            cross_a[h] = cross_c
            gvl_s[h] = nn(k2, above(c_hi, c_lo))
            gkl_s[h] = nt(beside(v, v), beside(c_hi, c_lo))
        else:
            k2, v = k2_s[0, h, :half], vc_s[0, h, :half]
            gv[h, rows[1]] = both[:half]
            gvl_bf[h, rows[1]] = (gvl_s[h] + both[half:]).astype(BF)
            cross[h] = (cross_a[h] + cross_c).astype(BF)
            gv_more[h] = nn(k2, above(c_hi, c_lo))
            gk_more[h] = nt(beside(v, v), beside(c_hi, c_lo))

    def key_part(c, h, which):
        y_hi, y_lo = split(y_s[c][h])
        part = slice(0, half) if which == 0 else slice(half, tok)
        scores = nn(k2_s[c, h, part], above(y_hi, y_lo))
        own = own_mask(half)
        scores = jnp.where(own, scores, 0.0) if which == 0 else jnp.where(own, 0.0, scores)
        a2_hi, a2_lo = split(vs_s[c, h, part] - scores)
        x_hi, x_lo = xs_s[h, rows[c], :DH], xs_s[h, rows[c], DH:]
        a1 = a1_s[c, h, part]
        g = nn(beside(a2_hi, a2_lo), above(x_hi, x_hi)) + nn(a2_hi, x_lo)
        return g - nt(a1, beside(y_hi, y_hi)) - nt(a1[:, :half], y_lo)

    def sym_part(c, h):
        y_hi, y_lo = split(-y_s[c][h])
        pair = nt(xt_s[c, h], beside(y_hi, y_hi)) + nt(xt_s[c, h, :, :half], y_lo)
        return pair + pair.T

    loop = ITERS // 2
    share = -(-heads // loop)

    def per_head(work):
        def run(i):
            for q in range(share):
                work(jnp.minimum(i * share + q, heads - 1) if share * loop > heads else i * share + q)
        return run

    def iterate(c, trips, extra):
        def step(i, carry):
            ps, pcs, sms, scs = [], [], [], []
            for h in range(heads):
                p = p_s[h]
                p_hi, p_lo = split(p)
                scs.append(nn(k2_s[c, h], above(p_hi, p_lo)))
                sms.append(nn(g_s[c, h], above(p_hi, p_lo)))
            images, curves = [], []
            for h in range(heads):
                p = p_s[h]
                scores = window_masked(scs[h])
                smooth = sms[h] + ridge[h] * p
                curve = jnp.sum(scores * scores, axis=0, keepdims=True)
                curves.append(curve + jnp.sum(p * smooth, axis=0, keepdims=True))
                images.append(nn(kt_s[c, h], scores.astype(BF)) + smooth)
            for h in range(heads):
                p = p_s[h]
                rr = rr_s[h]
                alpha = rr / (curves[h] + EPSILON)
                y_s[c][h] = y_s[c][h] + alpha * p
                r = r_s[h] - alpha * images[h]
                r_s[h] = r
                nr = jnp.sum(r * r, axis=0, keepdims=True)
                p_s[h] = r + nr / (rr + EPSILON) * p
                rr_s[h] = nr
            extra(i)
            return carry

        lax.fori_loop(0, trips, step, 0)

    def first_a(h):
        lag_scores(0, h)
        cross_part(0, h)

    def second_a(h):
        lag_scores(1, h)

    def first_b(h):
        cross_part(1, h)
        gkl_bf[h, rows[0]] = key_part(0, h, 1).astype(BF)

    def second_b(h):
        sy = sym_part(0, h)
        sym_a[h] = sy
        gkl_s[h] = gkl_s[h] + nn(k2_s[1, h, half:], above(*split(sy)))
        gk[h, rows[0]] = key_part(0, h, 0)
        gq[h, rows[0]] = y_s[0][h].T

    first, second = pl.ds(0, half), pl.ds(half, half)
    begin(0)
    iterate(0, loop, per_head(first_a))
    gva_hop = Hop(gvl_bf.at[:, first], gvl_in.at[:, first], -span).start()
    iterate(0, ITERS - loop, per_head(second_a))
    project(1)
    begin(1)
    iterate(1, loop, per_head(first_b))
    gvb_hop = Hop(gvl_bf.at[:, second], gvl_in.at[:, second], -span).start()
    cross_hops = mids(cross, cross_in, -1)
    gka_hop = Hop(gkl_bf.at[:, first], gkl_in.at[:, first], -span).start()
    iterate(1, ITERS - loop, per_head(second_b))
    for h in range(heads):
        gkl_bf[h, rows[1]] = (gkl_s[h] + key_part(1, h, 1)).astype(BF)
    gkb_hop = Hop(gkl_bf.at[:, second], gkl_in.at[:, second], -span).start()
    for h in range(heads):
        sy = sym_part(1, h)
        sym[h] = (sym_a[h] + sy).astype(BF)
        sym_a[h] = sy
    sym_hops = mids(sym, sym_in, -1)
    for h in range(heads):
        gk[h, rows[1]] = key_part(1, h, 0)
        more = gk_more[h] + nn(k2_s[0, h, :half], above(*split(sym_a[h])))
        gk[h, rows[0]] = gk[h, rows[0]] + more
        gv[h, rows[0]] = gv[h, rows[0]] + gv_more[h]
        gq[h, rows[1]] = y_s[1][h].T
    for hop in [gva_hop, gvb_hop] + cross_hops:
        hop.arrive()
    for h in range(heads):
        v_add = gvl_in[h].astype(F32)
        if span > 1:
            k, v = key[:, cols(h)], val[:, cols(h)]
            c_hi, c_lo = split(slots_sum(cross_in, h))
            v_add = v_add + nn(beside(k, k), above(c_hi, c_lo))
            gk[h] = gk[h] + nt(beside(v, v), beside(c_hi, c_lo))
        gv[h] = gv[h] + v_add
    for hop in [gka_hop, gkb_hop] + sym_hops:
        hop.arrive()
    for h in range(heads):
        k_add = gkl_in[h].astype(F32)
        if span > 1:
            k = key[:, cols(h)]
            k_add = k_add + nn(beside(k, k), above(*split(slots_sum(sym_in, h))))
        gk[h] = gk[h] + k_add
    for j in range(n_head):
        for c in range(2):
            pl.when(jnp.logical_and(has_right, j <= me))(lambda: d_copy(j, c, 1).wait_send())
            pl.when(jnp.logical_and(has_left, j >= me))(lambda: d_copy(j, c, -1).wait_send())
    for hop in hops:
        hop.finish()


def store(gq, gk, gv, gq_hbm, gk_hbm, gv_hbm, sem):
    copies = []
    for i, (source, target) in enumerate([(gq, gq_hbm), (gk, gk_hbm), (gv, gv_hbm)]):
        for h in range(source.shape[0]):
            copies.append(pltpu.make_async_copy(
                source.at[h], target.at[:, pl.ds(h * DH, DH)], sem.at[i, h]
            ))
    for copy in copies:
        copy.start()
    for copy in copies:
        copy.wait()


def body(key_rows, values, d_layer, out_weight, saved_solutions, ridge_scale):
    tok, cols = key_rows.shape
    heads = cols // DH
    half = tok // 2
    n_seq, n_head = lax.axis_size("seq"), lax.axis_size("head")
    span = n_seq // 4
    slots = max(span - 1, 1)
    copies = 6 + (4 if span == 2 else 3 * (span - 1))
    vmem = pl.BlockSpec(memory_space=pltpu.VMEM)
    hbm = pl.BlockSpec(memory_space=pltpu.HBM)
    flat = jax.ShapeDtypeStruct((tok, cols), F32)
    kept = pltpu.VMEM((heads, tok, DH), F32)
    rows_bf = pltpu.VMEM((tok, cols), BF)
    head_bf = pltpu.VMEM((heads, tok, DH), BF)
    mat_bf = pltpu.VMEM((heads, DH, DH), BF)
    mats_bf = pltpu.VMEM((heads, DH, 2 * DH), BF)
    mat_f = pltpu.VMEM((heads, DH, DH), F32)
    part_f = pltpu.VMEM((heads, half, DH), F32)
    vec = pltpu.VMEM((heads, DH, half), F32)
    results = pl.pallas_call(
        functools.partial(mega, span, n_seq, n_head),
        name="layer",
        out_shape=[kept, kept, kept],
        in_specs=[hbm] * 6,
        out_specs=[vmem, vmem, vmem],
        scratch_shapes=[
            pltpu.SMEM((heads,), F32), rows_bf, rows_bf, pltpu.VMEM((n_head,) + d_layer.shape, BF),
            pltpu.VMEM(out_weight.shape, BF), pltpu.VMEM((tok, cols), F32), rows_bf, rows_bf, head_bf,
            mats_bf, mats_bf, pltpu.VMEM((slots, heads, DH, 2 * DH), BF), mat_bf, mat_bf,
            pltpu.VMEM((slots, heads, DH, DH), BF), pltpu.VMEM((slots, heads, DH, DH), BF),
            head_bf, head_bf, head_bf, head_bf, part_f, part_f, part_f, part_f, mat_f, mat_f,
            pltpu.VMEM((2, heads, tok, 2 * DH), BF),
            pltpu.VMEM((2, heads, DH, tok), BF),
            pltpu.VMEM((2, heads, tok, DH), BF),
            pltpu.VMEM((heads, tok, 2 * DH), BF),
            pltpu.VMEM((2, heads, DH, tok), BF),
            pltpu.VMEM((2, heads, tok, tok), BF),
            pltpu.VMEM((2, heads, tok, half), F32),
            pltpu.VMEM((2, heads, DH, 2 * DH), F32),
            pltpu.VMEM((2, heads, DH, 2 * DH), BF),
            pltpu.VMEM((2, heads, DH, 2 * DH), BF),
            vec, vec, vec, vec,
            pltpu.VMEM((heads, 1, half), F32),
            pltpu.SemaphoreType.DMA((6,)),
            pltpu.SemaphoreType.DMA((4 * n_head,)),
            pltpu.SemaphoreType.DMA((2 * n_head,)),
            pltpu.SemaphoreType.DMA((copies,)),
            pltpu.SemaphoreType.DMA((copies,)),
        ],
        compiler_params=pltpu.CompilerParams(
            collective_id=0, has_side_effects=True, vmem_limit_bytes=48 * 1024 * 1024
        ),
    )(*(
        pltpu.with_memory_space_constraint(array, pltpu.HBM)
        for array in (ridge_scale, key_rows, values, d_layer, out_weight, saved_solutions)
    ))
    return pl.pallas_call(
        store,
        name="store",
        out_shape=[flat, flat, flat],
        in_specs=[vmem, vmem, vmem],
        out_specs=[hbm, hbm, hbm],
        scratch_shapes=[pltpu.SemaphoreType.DMA((3, heads))],
        compiler_params=pltpu.CompilerParams(vmem_limit_bytes=8 * 1024 * 1024),
    )(*(pltpu.with_memory_space_constraint(result, pltpu.VMEM) for result in results))


def solution(mesh):
    return jax.shard_map(
        body,
        mesh=mesh,
        in_specs=(
            P("seq", "head"),
            P("seq", "head"),
            P("seq", "head"),
            P("head", None),
            P("seq", "head"),
            P("head"),
        ),
        out_specs=(P("seq", "head"), P("seq", "head"), P("seq", "head")),
        check_vma=False,
    )
```

time: 51.5 us -> 45.8 us (0.89)
  the two profiles are of different devices: /device:TPU:11 before, /device:TPU:0 now
where the time goes in v2:
time: 45.8 us; the launch traced here: 44.9 us
  Pallas kernels  44.3 us (97%)
  between operations  0.64 us (1%)
    pallas_call x1, Pallas kernels, body(): pl.pallas_call(functools.partial(mega, span, n_seq, n_head), name='layer'...  43.1 us
    pallas_call x1, Pallas kernels, body(): pl.pallas_call(store, name='store', out_shape=[flat, flat, flat], in_spec...  1.24 us

profile of v2, /device:TPU:0, one launch (start us, length us, event | category | flops | bytes accessed | tf_op | source)
XLA Modules:
  0.0 44.9 jit_solution(11370156869174290327)
XLA Ops:
  0.6 43.1 %layer.1 = (f32[4,256,128]{2,1,0:T(8,128)S(1)}, f32[4,256,128]{2,1,0:T(8,128)S(1)}, f32[4,256,128]{2,1,0:T(8,128)S(1)}) custom-call(f32[4]{0:T(128)} %ridge_hbm.1, bf16[256,512]{1,0:T(8,128)(2,1)} %key_hbm.1, bf16[256,512]{1,0:T(8,128)(2,1)} %val_hbm.1, bf16[256,512]{1,0:T(8,128)(2,1)} %d_hbm.1, bf16[512,2048]{1,0:T(8,128)(2,1)} %w_hbm.1, f32[256,512]{1,0:T(8,128)} %sav_hbm.1), custom_call_target="tpu_custom_call" | custom-call | tf_op jit(solution)/shard_map/layer/pallas_call | solution.py:445
  43.7 1.2 %store.1 = (f32[256,512]{1,0:T(8,128)}, f32[256,512]{1,0:T(8,128)}, f32[256,512]{1,0:T(8,128)}) custom-call(f32[4,256,128]{2,1,0:T(8,128)S(1)} %get-tuple-element.6.gq, f32[4,256,128]{2,1,0:T(8,128)S(1)} %get-tuple-element.7.gk, f32[4,256,128]{2,1,0:T(8,128)S(1)} %get-tuple-element.8.gv), custom_call_target="tpu_custom_call" | custom-call | tf_op jit(solution)/shard_map/store/pallas_call | solution.py:482

commit v3 on v2

v3 whole, which is shorter than its diff:
```python
import functools
import jax
import jax.numpy as jnp
from jax import lax
from jax.experimental import pallas as pl
from jax.experimental.pallas import tpu as pltpu
from jax.sharding import PartitionSpec as P

DH = 128
ITERS = 8
PIECES = 4
EPSILON = 1e-06
BF = jnp.bfloat16
F32 = jnp.float32
MESH = pl.DeviceIdType.MESH


def nn(left, right):
    return lax.dot_general(left, right, (((1,), (0,)), ((), ())), preferred_element_type=F32)


def nt(left, right):
    return lax.dot_general(left, right, (((1,), (1,)), ((), ())), preferred_element_type=F32)


def split(a):
    hi = a.astype(BF)
    return hi, (a - hi.astype(F32)).astype(BF)


def flip(a):
    return a.astype(F32).T.astype(BF)


def beside(*parts):
    return jnp.concatenate(parts, axis=1)


def above(*parts):
    return jnp.concatenate(parts, axis=0)


def own_mask(tok):
    key_ids = lax.broadcasted_iota(jnp.int32, (tok, tok), 0)
    tok_ids = lax.broadcasted_iota(jnp.int32, (tok, tok), 1)
    return key_ids <= tok_ids


def window_masked(scores):
    tok = scores.shape[1]
    own = own_mask(tok)
    return above(jnp.where(own, scores[:tok], 0.0), jnp.where(own, 0.0, scores[tok:]))


def slots_sum(ref, h):
    total = ref[0, h].astype(F32)
    for slot in range(1, ref.shape[0]):
        total = total + ref[slot, h].astype(F32)
    return total


def mega(span, n_seq, n_head, ridge_hbm, key_hbm, val_hbm, d_hbm, w_hbm, sav_hbm, gq, gk, gv,
         ridge, key, val, d_all, w, sav, key_lag, val_lag, ot_s,
         mid, mid_lag, mid_in, cross, sym, cross_lead, sym_lead, cross_in, sym_in,
         x_bf, x_lead, o_lead, y_bf, y_lead,
         k2_s, kt_s, vc_s, xs_s, xt_s, a1_s, vs_s, full_s, g_s, st_s, r_s, p_s, ya_s, yb_s, rr_s,
         local_sem, dsend_sem, drecv_sem, send_sem, recv_sem):
    s = lax.axis_index("seq")
    me = lax.axis_index("head")
    heads = ridge.shape[0]
    tok = key.shape[0]
    half = tok // 2
    width = d_all.shape[2]
    rows = [slice(0, half), slice(half, tok)]
    pieces = [range(0, PIECES // 2), range(PIECES // 2, PIECES)]
    y_s = [ya_s, yb_s]
    d_copy_in = pltpu.make_async_copy(d_hbm, d_all.at[me], local_sem.at[0])
    key_copy = pltpu.make_async_copy(key_hbm, key, local_sem.at[1])
    val_copy = pltpu.make_async_copy(val_hbm, val, local_sem.at[2])
    w_copy = pltpu.make_async_copy(w_hbm, w, local_sem.at[3])
    x_copy = pltpu.make_async_copy(sav_hbm, sav, local_sem.at[4])
    ridge_copy = pltpu.make_async_copy(ridge_hbm, ridge, local_sem.at[5])
    for copy in (d_copy_in, key_copy, val_copy, x_copy, w_copy, ridge_copy):
        copy.start()

    def exists(d):
        return s + d < n_seq if d > 0 else s + d >= 0

    barrier = pltpu.get_barrier_semaphore()
    has_right, has_left = me + 1 < n_head, me > 0
    for there, step in ((has_right, 1), (has_left, -1)):
        @pl.when(there)
        def _():
            pl.semaphore_signal(barrier, inc=1, device_id={"head": me + step}, device_id_type=MESH)
    for d in [d for m in range(1, span + 1) for d in (m, -m)]:
        @pl.when(exists(d))
        def _():
            pl.semaphore_signal(barrier, inc=1, device_id={"seq": s + d}, device_id_type=MESH)
    pl.semaphore_wait(
        barrier,
        jnp.minimum(me, 1) + jnp.minimum(n_head - 1 - me, 1)
        + jnp.minimum(s, span) + jnp.minimum(n_seq - 1 - s, span),
    )

    counter = [0]
    hops = []

    class Hop:
        def __init__(self, source, target, d, sender=None, receiver=None):
            self.sender = exists(d) if sender is None else sender
            self.receiver = exists(-d) if receiver is None else receiver
            self.copy = pltpu.make_async_remote_copy(
                src_ref=source,
                dst_ref=target,
                send_sem=send_sem.at[counter[0]],
                recv_sem=recv_sem.at[counter[0]],
                device_id={"seq": s + d},
                device_id_type=MESH,
            )
            counter[0] += 1
            hops.append(self)
            if receiver is None:
                @pl.when(jnp.logical_not(self.receiver))
                def _():
                    target[...] = jnp.zeros(target.shape, target.dtype)

        def start(self):
            pl.when(self.sender)(self.copy.start)
            return self

        def arrive(self):
            pl.when(self.receiver)(self.copy.wait_recv)

        def finish(self):
            pl.when(self.sender)(self.copy.wait_send)

    def mids(source, target, sign):
        return [Hop(source, target.at[m - 1], sign * m).start() for m in range(1, span)]

    def d_copy(origin, q, step):
        piece = d_all.at[origin, pl.ds(q * (tok // PIECES), tok // PIECES)]
        place = origin * PIECES + q
        return pltpu.make_async_remote_copy(
            src_ref=piece,
            dst_ref=piece,
            send_sem=dsend_sem.at[place + (0 if step > 0 else PIECES * n_head)],
            recv_sem=drecv_sem.at[place],
            device_id={"head": me + step},
            device_id_type=MESH,
        )

    def d_start(q):
        pl.when(has_right)(lambda: d_copy(me, q, 1).start())
        pl.when(has_left)(lambda: d_copy(me, q, -1).start())

    def d_relay(k, q):
        @pl.when(jnp.logical_and(me - k >= 0, has_right))
        def _():
            copy = d_copy(me - k, q, 1)
            copy.wait_recv()
            copy.start()

        @pl.when(jnp.logical_and(me + k < n_head, has_left))
        def _():
            copy = d_copy(me + k, q, -1)
            copy.wait_recv()
            copy.start()

    at_end = jnp.logical_or(me == 0, me == n_head - 1)

    def project(c):
        acc = None
        for i in range(n_head):
            origin = jnp.where(me == 0, i, n_head - 1 - i)
            if i:
                @pl.when(at_end)
                def _():
                    for q in pieces[c]:
                        d_copy(origin, q, 1).wait_recv()
            col = pl.multiple_of(origin * width, width)
            part = nt(w[:, pl.ds(col, width)], d_all[origin, rows[c]])
            acc = part if acc is None else acc + part
        for h in range(heads):
            ot_s[c, h] = acc[h * DH : (h + 1) * DH].astype(BF)

    def cols(h):
        return slice(h * DH, (h + 1) * DH)

    d_copy_in.wait()
    for q in pieces[0]:
        d_start(q)
    key_copy.wait()
    key_hop = Hop(key, key_lag, span).start()
    val_copy.wait()
    val_hop = Hop(val, val_lag, span).start()
    for h in range(heads):
        total = None
        for c in range(2):
            k, v = key[rows[c], cols(h)], val[rows[c], cols(h)]
            kt = flip(k)
            kt_s[c, h, :, :half] = kt
            k2_s[c, h, :half] = beside(k, k)
            vc_s[c, h, :half] = v
            both = nn(kt, beside(k, v))
            if c == 0:
                full_s[1, h] = both
            total = both if total is None else total + both
        mid[h] = total.astype(BF)
    paired = span == 2
    if paired:
        odd = lax.rem(s, 2) == 1
        even = jnp.logical_not(odd)
        mid_hops = [Hop(mid, mid_in.at[0], 1, even, odd).start()]
    else:
        mid_hops = mids(mid, mid_in, 1)
    x_copy.wait()
    for h in range(heads):
        x_hi, x_lo = split(sav[:, cols(h)])
        x_bf[h] = x_hi
        xs_s[h] = beside(x_hi, x_lo)
    x_hop = Hop(x_bf, x_lead, -span).start()
    for h in range(heads):
        for c in range(2):
            xt_s[c, h] = beside(*split(sav[rows[c], cols(h)].T))
            scores = nt(k2_s[c, h, :half], xs_s[h, rows[c]])
            a1_s[c, h] = beside(*split(jnp.where(own_mask(half), scores, 0.0)))
    late = list(pieces[1])
    for k in range(1, max(n_head - 1, len(late) + 1)):
        if k < n_head - 1:
            for q in pieces[0]:
                d_relay(k, q)
        if late:
            d_start(late.pop(0))
    if n_head > 2:
        for q in pieces[1]:
            d_relay(1, q)
    w_copy.wait()
    ridge_copy.wait()
    project(0)
    key_hop.arrive()
    for h in range(heads):
        for c in range(2):
            k = key_lag[rows[c], cols(h)]
            kt_s[c, h, :, half:] = flip(k)
            k2_s[c, h, half:] = beside(k, k)
    val_hop.arrive()
    for h in range(heads):
        for c in range(2):
            vc_s[c, h, half:] = val_lag[rows[c], cols(h)]
        late = nn(kt_s[1, h, :, half:], beside(k2_s[1, h, half:, :DH], vc_s[1, h, half:]))
        full_s[0, h] = late
        if paired:
            early = nn(kt_s[0, h, :, half:], beside(k2_s[0, h, half:, :DH], vc_s[0, h, half:]))
            mid_lag[h] = (early + late).astype(BF)
    if paired:
        mid_hops.append(Hop(mid_lag, mid_in.at[0], -1, odd, even).start())
    for k in range(2, n_head - 1):
        for q in pieces[1]:
            d_relay(k, q)
    pl.when(jnp.logical_not(at_end))(lambda: project(1))
    for hop in mid_hops:
        hop.arrive()
    for h in range(heads):
        for c in range(2):
            total = full_s[c, h]
            if span > 1:
                total = total + slots_sum(mid_in, h)
            g_hi, g_lo = split(total[:, :DH])
            g_s[c, h] = beside(g_hi, g_hi)
            st_s[c, h] = beside(*split(total[:, DH:]))

    def begin(c):
        outs = [ot_s[c, h] for h in range(heads)]
        scores = [nn(vc_s[c, h], outs[h]) for h in range(heads)]
        base = [nn(st_s[c, h], above(outs[h], outs[h])) for h in range(heads)]
        parts = []
        for h in range(heads):
            masked = window_masked(scores[h])
            vs_s[c, h] = masked[:half]
            parts.append(split(masked))
        rs = [base[h] + nn(kt_s[c, h], parts[h][0]) + nn(kt_s[c, h], parts[h][1]) for h in range(heads)]
        for h in range(heads):
            r_s[h] = rs[h]
            p_s[h] = rs[h]
            y_s[c][h] = jnp.zeros_like(rs[h])
            rr_s[h] = jnp.sum(rs[h] * rs[h], axis=0, keepdims=True)

    def iterate(c):
        def step(i, carry):
            smooths, scores = [], []
            for h in range(heads):
                p_hi, p_lo = split(p_s[h])
                p2 = above(p_hi, p_lo)
                scores.append(nn(k2_s[c, h], p2))
                smooths.append(nn(g_s[c, h], p2))
            images, curves = [], []
            for h in range(heads):
                p = p_s[h]
                masked = window_masked(scores[h])
                smooth = smooths[h] + ridge[h] * p
                curve = jnp.sum(masked * masked, axis=0, keepdims=True)
                curves.append(curve + jnp.sum(p * smooth, axis=0, keepdims=True))
                images.append(nn(kt_s[c, h], masked.astype(BF)) + smooth)
            for h in range(heads):
                p = p_s[h]
                rr = rr_s[h]
                alpha = rr / (curves[h] + EPSILON)
                y_s[c][h] = y_s[c][h] + alpha * p
                r = r_s[h] - alpha * images[h]
                r_s[h] = r
                nr = jnp.sum(r * r, axis=0, keepdims=True)
                p_s[h] = r + nr / (rr + EPSILON) * p
                rr_s[h] = nr
            return carry

        lax.fori_loop(0, ITERS, step, 0)
        for h in range(heads):
            y_bf[c, h] = y_s[c][h].astype(BF)

    every = list(range(heads))

    def twice(a):
        return beside(a, a)

    def negative_sym(pair):
        return -(pair + pair.T)

    def apply_states(c_f, s_f, k, v):
        c_hi, c_lo = split(c_f)
        to_k = nt(twice(v), beside(c_hi, c_lo))
        if s_f is not None:
            to_k = to_k + nn(twice(k), above(*split(s_f)))
        return to_k, nn(twice(k), above(c_hi, c_lo))

    o_hops = [Hop(ot_s.at[0], o_lead.at[0], -span).start()]
    begin(0)
    iterate(0)
    y_hops = [Hop(y_bf.at[0], y_lead.at[0], -span).start()]
    pl.when(at_end)(lambda: project(1))
    o_hops.append(Hop(ot_s.at[1], o_lead.at[1], -span).start())
    begin(1)
    iterate(1)
    y_hops.append(Hop(y_bf.at[1], y_lead.at[1], -span).start())

    crosses = [[nt(xt_s[c, h], twice(ot_s[c, h])) for h in every] for c in range(2)]
    pairs = [[], []]
    for c in range(2):
        for h in every:
            y_hi, y_lo = split(y_s[c][h])
            pairs[c].append(nt(xt_s[c, h], twice(y_hi)) + nt(xt_s[c, h, :, :half], y_lo))
    for h in every:
        cross[h] = (crosses[0][h] + crosses[1][h]).astype(BF)
        sym[h] = negative_sym(pairs[0][h] + pairs[1][h]).astype(BF)
    if paired:
        state_hops = [
            Hop(cross, cross_in.at[0], -1, odd, even).start(), Hop(sym, sym_in.at[0], -1, odd, even).start()
        ]
    else:
        state_hops = mids(cross, cross_in, -1) + mids(sym, sym_in, -1)
    for h in every:
        to_k, to_v = apply_states(
            crosses[1][h], negative_sym(pairs[1][h]), k2_s[0, h, :half, :DH], vc_s[0, h, :half]
        )
        gk[h, rows[0]] = to_k
        gv[h, rows[0]] = to_v + nt(a1_s[0, h], twice(ot_s[0, h]))
        gv[h, rows[1]] = nt(a1_s[1, h], twice(ot_s[1, h]))
    own = own_mask(half)
    for c in range(2):
        ys = [split(y_s[c][h]) for h in every]
        scores = [nn(k2_s[c, h, :half], above(*ys[h])) for h in every]
        for h in every:
            y_hi, y_lo = ys[h]
            a2_hi, a2_lo = split(vs_s[c, h] - jnp.where(own, scores[h], 0.0))
            x_hi, x_lo = xs_s[h, rows[c], :DH], xs_s[h, rows[c], DH:]
            a1 = a1_s[c, h]
            g = nn(beside(a2_hi, a2_lo), above(x_hi, x_hi)) + nn(a2_hi, x_lo)
            g = g - nt(a1, twice(y_hi)) - nt(a1[:, :half], y_lo)
            gk[h, rows[c]] = gk[h, rows[c]] + g if c == 0 else g
    for h in every:
        for c in range(2):
            gq[h, rows[c]] = y_s[c][h].T

    x_hop.arrive()
    for hop in o_hops:
        hop.arrive()
    seen = []
    for c in range(2):
        scores = [nt(k2_s[c, h, :half, :DH], x_lead[h, rows[c]]) for h in every]
        seen.append([beside(*split(jnp.where(own, 0.0, t))) for t in scores])
        for h in every:
            gv[h, rows[c]] = gv[h, rows[c]] + nt(seen[c][h], twice(o_lead[c, h]))
    flipped = [[flip(x_lead[h, rows[c]]) for h in every] for c in range(2)]
    crosses = [[nt(flipped[c][h], o_lead[c, h]) for h in every] for c in range(2)]
    if paired:
        for h in every:
            cross_lead[h] = (crosses[0][h] + crosses[1][h]).astype(BF)
        state_hops.append(Hop(cross_lead, cross_in.at[0], 1, even, odd).start())

    def lead_part(c):
        scores = []
        for h in every:
            vk = beside(vc_s[c, h, :half], k2_s[c, h, :half, :DH])
            scores.append(nn(vk, above(o_lead[c, h], -y_lead[c, h])))
        for h in every:
            a2_hi, a2_lo = split(jnp.where(own, 0.0, scores[h]))
            x = x_lead[h, rows[c]]
            g = nn(beside(a2_hi, a2_lo), above(x, x)) - nt(seen[c][h], twice(y_lead[c, h]))
            gk[h, rows[c]] = gk[h, rows[c]] + g

    y_hops[0].arrive()
    pairs = [nt(flipped[0][h], y_lead[0, h]) for h in every]
    for h in every:
        to_k, to_v = apply_states(crosses[0][h], negative_sym(pairs[h]), k2_s[1, h, :half, :DH], vc_s[1, h, :half])
        gk[h, rows[1]] = gk[h, rows[1]] + to_k
        gv[h, rows[1]] = gv[h, rows[1]] + to_v
    lead_part(0)
    y_hops[1].arrive()
    if paired:
        lates = [nt(flipped[1][h], y_lead[1, h]) for h in every]
        for h in every:
            sym_lead[h] = negative_sym(pairs[h] + lates[h]).astype(BF)
        state_hops.append(Hop(sym_lead, sym_in.at[0], 1, even, odd).start())
    lead_part(1)
    for hop in state_hops:
        hop.arrive()
    if span > 1:
        for h in every:
            c_f, s_f = slots_sum(cross_in, h), slots_sum(sym_in, h)
            to_k, to_v = apply_states(c_f, s_f, key[:, cols(h)], val[:, cols(h)])
            gk[h] = gk[h] + to_k
            gv[h] = gv[h] + to_v
    for j in range(n_head):
        @pl.when(jnp.logical_and(has_right, j <= me))
        def _():
            for q in range(PIECES):
                d_copy(j, q, 1).wait_send()

        @pl.when(jnp.logical_and(has_left, j >= me))
        def _():
            for q in range(PIECES):
                d_copy(j, q, -1).wait_send()
    for hop in hops:
        hop.finish()


def store(gq, gk, gv, gq_hbm, gk_hbm, gv_hbm, sem):
    copies = []
    for i, (source, target) in enumerate([(gq, gq_hbm), (gk, gk_hbm), (gv, gv_hbm)]):
        for h in range(source.shape[0]):
            copies.append(pltpu.make_async_copy(
                source.at[h], target.at[:, pl.ds(h * DH, DH)], sem.at[i, h]
            ))
    for copy in copies:
        copy.start()
    for copy in copies:
        copy.wait()


def body(key_rows, values, d_layer, out_weight, saved_solutions, ridge_scale):
    tok, cols = key_rows.shape
    heads = cols // DH
    half = tok // 2
    n_seq, n_head = lax.axis_size("seq"), lax.axis_size("head")
    span = n_seq // 4
    slots = max(span - 1, 1)
    copies = 7 + (6 if span == 2 else 3 * (span - 1))
    vmem = pl.BlockSpec(memory_space=pltpu.VMEM)
    hbm = pl.BlockSpec(memory_space=pltpu.HBM)
    flat = jax.ShapeDtypeStruct((tok, cols), F32)
    kept = pltpu.VMEM((heads, tok, DH), F32)
    rows_bf = pltpu.VMEM((tok, cols), BF)
    head_bf = pltpu.VMEM((heads, tok, DH), BF)
    mat_bf = pltpu.VMEM((heads, DH, DH), BF)
    mats_bf = pltpu.VMEM((heads, DH, 2 * DH), BF)
    turned_bf = pltpu.VMEM((2, heads, DH, half), BF)
    vec = pltpu.VMEM((heads, DH, half), F32)
    results = pl.pallas_call(
        functools.partial(mega, span, n_seq, n_head),
        name="layer",
        out_shape=[kept, kept, kept],
        in_specs=[hbm] * 6,
        out_specs=[vmem, vmem, vmem],
        scratch_shapes=[
            pltpu.SMEM((heads,), F32), rows_bf, rows_bf, pltpu.VMEM((n_head,) + d_layer.shape, BF),
            pltpu.VMEM(out_weight.shape, BF), pltpu.VMEM((tok, cols), F32), rows_bf, rows_bf, turned_bf,
            mats_bf, mats_bf, pltpu.VMEM((slots, heads, DH, 2 * DH), BF), mat_bf, mat_bf, mat_bf, mat_bf,
            pltpu.VMEM((slots, heads, DH, DH), BF), pltpu.VMEM((slots, heads, DH, DH), BF),
            head_bf, head_bf, turned_bf, turned_bf, turned_bf,
            pltpu.VMEM((2, heads, tok, 2 * DH), BF),
            pltpu.VMEM((2, heads, DH, tok), BF),
            pltpu.VMEM((2, heads, tok, DH), BF),
            pltpu.VMEM((heads, tok, 2 * DH), BF),
            pltpu.VMEM((2, heads, DH, tok), BF),
            pltpu.VMEM((2, heads, half, tok), BF),
            pltpu.VMEM((2, heads, half, half), F32),
            pltpu.VMEM((2, heads, DH, 2 * DH), F32),
            pltpu.VMEM((2, heads, DH, 2 * DH), BF),
            pltpu.VMEM((2, heads, DH, 2 * DH), BF),
            vec, vec, vec, vec,
            pltpu.VMEM((heads, 1, half), F32),
            pltpu.SemaphoreType.DMA((6,)),
            pltpu.SemaphoreType.DMA((2 * PIECES * n_head,)),
            pltpu.SemaphoreType.DMA((PIECES * n_head,)),
            pltpu.SemaphoreType.DMA((copies,)),
            pltpu.SemaphoreType.DMA((copies,)),
        ],
        compiler_params=pltpu.CompilerParams(
            collective_id=0, has_side_effects=True, vmem_limit_bytes=48 * 1024 * 1024
        ),
    )(*(
        pltpu.with_memory_space_constraint(array, pltpu.HBM)
        for array in (ridge_scale, key_rows, values, d_layer, out_weight, saved_solutions)
    ))
    return pl.pallas_call(
        store,
        name="store",
        out_shape=[flat, flat, flat],
        in_specs=[vmem, vmem, vmem],
        out_specs=[hbm, hbm, hbm],
        scratch_shapes=[pltpu.SemaphoreType.DMA((3, heads))],
        compiler_params=pltpu.CompilerParams(vmem_limit_bytes=8 * 1024 * 1024),
    )(*(pltpu.with_memory_space_constraint(result, pltpu.VMEM) for result in results))


def solution(mesh):
    return jax.shard_map(
        body,
        mesh=mesh,
        in_specs=(
            P("seq", "head"),
            P("seq", "head"),
            P("seq", "head"),
            P("head", None),
            P("seq", "head"),
            P("head"),
        ),
        out_specs=(P("seq", "head"), P("seq", "head"), P("seq", "head")),
        check_vma=False,
    )
```

time: 45.8 us -> 38.9 us (0.85)
  Pallas kernels: 44.3 us -> 37.5 us
    pallas_call x1, Pallas kernels: 43.1 us -> 36.3 us  [body(): pl.pallas_call(functools.partial(mega, span, n_seq, n_head), name='layer'...]
where the time goes in v3:
time: 38.9 us; the launch traced here: 38.1 us
  Pallas kernels  37.5 us (96%)
  between operations  0.64 us (2%)
    pallas_call x1, Pallas kernels, body(): pl.pallas_call(functools.partial(mega, span, n_seq, n_head), name='layer'...  36.3 us
    pallas_call x1, Pallas kernels, body(): pl.pallas_call(store, name='store', out_shape=[flat, flat, flat], in_spec...  1.24 us

profile of v3, /device:TPU:0, one launch (start us, length us, event | category | flops | bytes accessed | tf_op | source)
XLA Modules:
  0.0 38.1 jit_solution(11139157143607672417)
XLA Ops:
  0.6 36.3 %layer.1 = (f32[4,256,128]{2,1,0:T(8,128)S(1)}, f32[4,256,128]{2,1,0:T(8,128)S(1)}, f32[4,256,128]{2,1,0:T(8,128)S(1)}) custom-call(f32[4]{0:T(128)} %ridge_hbm.1, bf16[256,512]{1,0:T(8,128)(2,1)} %key_hbm.1, bf16[256,512]{1,0:T(8,128)(2,1)} %val_hbm.1, bf16[256,512]{1,0:T(8,128)(2,1)} %d_hbm.1, bf16[512,2048]{1,0:T(8,128)(2,1)} %w_hbm.1, f32[256,512]{1,0:T(8,128)} %sav_hbm.1), custom_call_target="tpu_custom_call" | custom-call | tf_op jit(solution)/shard_map/layer/pallas_call | solution.py:477
  36.9 1.2 %store.1 = (f32[256,512]{1,0:T(8,128)}, f32[256,512]{1,0:T(8,128)}, f32[256,512]{1,0:T(8,128)}) custom-call(f32[4,256,128]{2,1,0:T(8,128)S(1)} %get-tuple-element.6.gq, f32[4,256,128]{2,1,0:T(8,128)S(1)} %get-tuple-element.7.gk, f32[4,256,128]{2,1,0:T(8,128)S(1)} %get-tuple-element.8.gv), custom_call_target="tpu_custom_call" | custom-call | tf_op jit(solution)/shard_map/store/pallas_call | solution.py:514

commit v4 on v3

--- a/solution.py
+++ b/solution.py
@@ -59,11 +59,11 @@
     return total
 
 
-def mega(span, n_seq, n_head, ridge_hbm, key_hbm, val_hbm, d_hbm, w_hbm, sav_hbm, gq, gk, gv,
+def mega(span, n_seq, n_head, ridge_hbm, key_hbm, val_hbm, d_hbm, w_hbm, sav_hbm, gq, gk, gv, key_out, sym_out,
          ridge, key, val, d_all, w, sav, key_lag, val_lag, ot_s,
          mid, mid_lag, mid_in, cross, sym, cross_lead, sym_lead, cross_in, sym_in,
-         x_bf, x_lead, o_lead, y_bf, y_lead,
-         k2_s, kt_s, vc_s, xs_s, xt_s, a1_s, vs_s, full_s, g_s, st_s, r_s, p_s, ya_s, yb_s, rr_s,
+         x_bf, x_lead, o_lead, y_bf, y_lead, key_stop, val_stop, x_stop, o_stop,
+         k2_s, kt_s, vc_s, xs_s, xt_s, a1_s, vs_s, full_s, g_s, st_s, r_s, p_s, p2_s, ya_s, yb_s, rr_s,
          local_sem, dsend_sem, drecv_sem, send_sem, recv_sem):
     s = lax.axis_index("seq")
     me = lax.axis_index("head")
@@ -86,6 +86,10 @@
     def exists(d):
         return s + d < n_seq if d > 0 else s + d >= 0
 
+    paired = span == 2
+    odd = lax.rem(s, 2) == 1
+    even = jnp.logical_not(odd)
+    detour = paired and n_seq == 8
     barrier = pltpu.get_barrier_semaphore()
     has_right, has_left = me + 1 < n_head, me > 0
     for there, step in ((has_right, 1), (has_left, -1)):
@@ -96,8 +100,14 @@
         @pl.when(exists(d))
         def _():
             pl.semaphore_signal(barrier, inc=1, device_id={"seq": s + d}, device_id_type=MESH)
+    if detour:
+        @pl.when(odd)
+        def _():
+            far = lax.rem(s + n_seq // 2, n_seq)
+            pl.semaphore_signal(barrier, inc=1, device_id={"seq": far}, device_id_type=MESH)
     pl.semaphore_wait(
         barrier,
+        (lax.rem(s, 2) if detour else 0) +
         jnp.minimum(me, 1) + jnp.minimum(n_head - 1 - me, 1)
         + jnp.minimum(s, span) + jnp.minimum(n_seq - 1 - s, span),
     )
@@ -106,9 +116,12 @@
     hops = []
 
     class Hop:
-        def __init__(self, source, target, d, sender=None, receiver=None):
+        def __init__(self, source, target, d, sender=None, receiver=None, skip=None):
             self.sender = exists(d) if sender is None else sender
             self.receiver = exists(-d) if receiver is None else receiver
+            if skip is not None:
+                self.sender = jnp.logical_and(self.sender, s != skip[0])
+                self.receiver = jnp.logical_and(self.receiver, s != skip[1])
             self.copy = pltpu.make_async_remote_copy(
                 src_ref=source,
                 dst_ref=target,
@@ -120,7 +133,7 @@
             counter[0] += 1
             hops.append(self)
             if receiver is None:
-                @pl.when(jnp.logical_not(self.receiver))
+                @pl.when(jnp.logical_not(exists(-d)))
                 def _():
                     target[...] = jnp.zeros(target.shape, target.dtype)
 
@@ -133,6 +146,28 @@
 
         def finish(self):
             pl.when(self.sender)(self.copy.wait_send)
+
+    class Route:
+        def __init__(self, source, target, d, stop):
+            a, b = n_seq // 2 - d // 2, n_seq // 2 + d // 2
+            way = (a + n_seq // 2) % n_seq
+            self.direct = Hop(source, target, d, skip=(a, b) if detour else None).start()
+            self.legs = []
+            if detour:
+                self.legs = [
+                    Hop(source, stop, way - a, s == a, s == way).start(),
+                    Hop(stop, target, b - way, s == way, s == b),
+                ]
+
+        def forward(self):
+            if self.legs:
+                self.legs[0].arrive()
+                self.legs[1].start()
+
+        def arrive(self):
+            self.direct.arrive()
+            if self.legs:
+                self.legs[1].arrive()
 
     def mids(source, target, sign):
         return [Hop(source, target.at[m - 1], sign * m).start() for m in range(1, span)]
@@ -190,9 +225,9 @@
     for q in pieces[0]:
         d_start(q)
     key_copy.wait()
-    key_hop = Hop(key, key_lag, span).start()
+    key_hop = Route(key, key_lag, span, key_stop)
     val_copy.wait()
-    val_hop = Hop(val, val_lag, span).start()
+    val_hop = Route(val, val_lag, span, val_stop)
     for h in range(heads):
         total = None
         for c in range(2):
@@ -206,10 +241,7 @@
                 full_s[1, h] = both
             total = both if total is None else total + both
         mid[h] = total.astype(BF)
-    paired = span == 2
     if paired:
-        odd = lax.rem(s, 2) == 1
-        even = jnp.logical_not(odd)
         mid_hops = [Hop(mid, mid_in.at[0], 1, even, odd).start()]
     else:
         mid_hops = mids(mid, mid_in, 1)
@@ -218,7 +250,7 @@
         x_hi, x_lo = split(sav[:, cols(h)])
         x_bf[h] = x_hi
         xs_s[h] = beside(x_hi, x_lo)
-    x_hop = Hop(x_bf, x_lead, -span).start()
+    x_hop = Route(x_bf, x_lead, -span, x_stop)
     for h in range(heads):
         for c in range(2):
             xt_s[c, h] = beside(*split(sav[rows[c], cols(h)].T))
@@ -231,12 +263,20 @@
                 d_relay(k, q)
         if late:
             d_start(late.pop(0))
-    if n_head > 2:
-        for q in pieces[1]:
-            d_relay(1, q)
+        if k == 1:
+            key_hop.forward()
+    val_hop.forward()
+    x_hop.forward()
+    rest = [(k, q) for k in range(1, n_head - 1) for q in pieces[1]]
+    for k, q in rest[:2]:
+        d_relay(k, q)
+    rest = rest[2:]
+    for h in range(heads):
+        key_out[h] = key[:, cols(h)]
     w_copy.wait()
     ridge_copy.wait()
     project(0)
+    o_hops = [Route(ot_s.at[0], o_lead.at[0], -span, o_stop)]
     key_hop.arrive()
     for h in range(heads):
         for c in range(2):
@@ -254,10 +294,8 @@
             mid_lag[h] = (early + late).astype(BF)
     if paired:
         mid_hops.append(Hop(mid_lag, mid_in.at[0], -1, odd, even).start())
-    for k in range(2, n_head - 1):
-        for q in pieces[1]:
-            d_relay(k, q)
-    pl.when(jnp.logical_not(at_end))(lambda: project(1))
+    for k, q in rest[: len(rest) // 2]:
+        d_relay(k, q)
     for hop in mid_hops:
         hop.arrive()
     for h in range(heads):
@@ -282,40 +320,54 @@
         for h in range(heads):
             r_s[h] = rs[h]
             p_s[h] = rs[h]
+            p2_s[h] = above(*split(rs[h]))
             y_s[c][h] = jnp.zeros_like(rs[h])
             rr_s[h] = jnp.sum(rs[h] * rs[h], axis=0, keepdims=True)
 
-    def iterate(c):
-        def step(i, carry):
+    def iterate(c, between=None):
+        def curves():
             smooths, scores = [], []
             for h in range(heads):
-                p_hi, p_lo = split(p_s[h])
-                p2 = above(p_hi, p_lo)
-                scores.append(nn(k2_s[c, h], p2))
-                smooths.append(nn(g_s[c, h], p2))
-            images, curves = [], []
+                scores.append(nn(k2_s[c, h], p2_s[h]))
+                smooths.append(nn(g_s[c, h], p2_s[h]))
+            result = []
             for h in range(heads):
                 p = p_s[h]
                 masked = window_masked(scores[h])
                 smooth = smooths[h] + ridge[h] * p
                 curve = jnp.sum(masked * masked, axis=0, keepdims=True)
-                curves.append(curve + jnp.sum(p * smooth, axis=0, keepdims=True))
-                images.append(nn(kt_s[c, h], masked.astype(BF)) + smooth)
+                curve = curve + jnp.sum(p * smooth, axis=0, keepdims=True)
+                result.append((masked, smooth, curve + EPSILON))
+            return result
+
+        def step(i, carry):
+            found = curves()
+            images = [nn(kt_s[c, h], found[h][0].astype(BF)) + found[h][1] for h in range(heads)]
             for h in range(heads):
                 p = p_s[h]
                 rr = rr_s[h]
-                alpha = rr / (curves[h] + EPSILON)
+                alpha = rr / found[h][2]
                 y_s[c][h] = y_s[c][h] + alpha * p
                 r = r_s[h] - alpha * images[h]
                 r_s[h] = r
                 nr = jnp.sum(r * r, axis=0, keepdims=True)
-                p_s[h] = r + nr / (rr + EPSILON) * p
+                p = r + nr / (rr + EPSILON) * p
+                p_s[h] = p
+                p2_s[h] = above(*split(p))
                 rr_s[h] = nr
             return carry
 
-        lax.fori_loop(0, ITERS, step, 0)
+        if between is None:
+            lax.fori_loop(0, ITERS - 1, step, 0)
+        else:
+            lax.fori_loop(0, ITERS // 2, step, 0)
+            between()
+            lax.fori_loop(ITERS // 2, ITERS - 1, step, 0)
+        found = curves()
         for h in range(heads):
-            y_bf[c, h] = y_s[c][h].astype(BF)
+            y = y_s[c][h] + rr_s[h] / found[h][2] * p_s[h]
+            y_s[c][h] = y
+            y_bf[c, h] = y.astype(BF)
 
     every = list(range(heads))
 
@@ -332,11 +384,21 @@
             to_k = to_k + nn(twice(k), above(*split(s_f)))
         return to_k, nn(twice(k), above(c_hi, c_lo))
 
-    o_hops = [Hop(ot_s.at[0], o_lead.at[0], -span).start()]
+    def apply_cross():
+        for h in every:
+            to_k, to_v = apply_states(slots_sum(cross_in, h), None, key[:, cols(h)], val[:, cols(h)])
+            gk[h] = gk[h] + to_k
+            gv[h] = gv[h] + to_v
+
+    def halfway():
+        for k, q in rest[len(rest) // 2 :]:
+            d_relay(k, q)
+        o_hops[0].forward()
+
     begin(0)
-    iterate(0)
+    iterate(0, halfway)
     y_hops = [Hop(y_bf.at[0], y_lead.at[0], -span).start()]
-    pl.when(at_end)(lambda: project(1))
+    project(1)
     o_hops.append(Hop(ot_s.at[1], o_lead.at[1], -span).start())
     begin(1)
     iterate(1)
@@ -352,11 +414,10 @@
         cross[h] = (crosses[0][h] + crosses[1][h]).astype(BF)
         sym[h] = negative_sym(pairs[0][h] + pairs[1][h]).astype(BF)
     if paired:
-        state_hops = [
-            Hop(cross, cross_in.at[0], -1, odd, even).start(), Hop(sym, sym_in.at[0], -1, odd, even).start()
-        ]
+        cross_hops = [Hop(cross, cross_in.at[0], -1, odd, even).start()]
+        sym_hops = [Hop(sym, sym_in.at[0], -1, odd, even).start()]
     else:
-        state_hops = mids(cross, cross_in, -1) + mids(sym, sym_in, -1)
+        cross_hops, sym_hops = mids(cross, cross_in, -1), mids(sym, sym_in, -1)
     for h in every:
         to_k, to_v = apply_states(
             crosses[1][h], negative_sym(pairs[1][h]), k2_s[0, h, :half, :DH], vc_s[0, h, :half]
@@ -394,7 +455,7 @@
     if paired:
         for h in every:
             cross_lead[h] = (crosses[0][h] + crosses[1][h]).astype(BF)
-        state_hops.append(Hop(cross_lead, cross_in.at[0], 1, even, odd).start())
+        cross_hops.append(Hop(cross_lead, cross_in.at[0], 1, even, odd).start())
 
     def lead_part(c):
         scores = []
@@ -414,21 +475,21 @@
         gk[h, rows[1]] = gk[h, rows[1]] + to_k
         gv[h, rows[1]] = gv[h, rows[1]] + to_v
     lead_part(0)
+    for hop in cross_hops:
+        hop.arrive()
+    if span > 1:
+        apply_cross()
     y_hops[1].arrive()
     if paired:
         lates = [nt(flipped[1][h], y_lead[1, h]) for h in every]
         for h in every:
             sym_lead[h] = negative_sym(pairs[h] + lates[h]).astype(BF)
-        state_hops.append(Hop(sym_lead, sym_in.at[0], 1, even, odd).start())
+        sym_hops.append(Hop(sym_lead, sym_in.at[0], 1, even, odd).start())
     lead_part(1)
-    for hop in state_hops:
+    for hop in sym_hops:
         hop.arrive()
-    if span > 1:
-        for h in every:
-            c_f, s_f = slots_sum(cross_in, h), slots_sum(sym_in, h)
-            to_k, to_v = apply_states(c_f, s_f, key[:, cols(h)], val[:, cols(h)])
-            gk[h] = gk[h] + to_k
-            gv[h] = gv[h] + to_v
+    for h in every:
+        sym_out[h] = above(*split(slots_sum(sym_in, h))) if span > 1 else jnp.zeros(sym_out.shape[1:], BF)
     for j in range(n_head):
         @pl.when(jnp.logical_and(has_right, j <= me))
         def _():
@@ -443,16 +504,24 @@
         hop.finish()
 
 
-def store(gq, gk, gv, gq_hbm, gk_hbm, gv_hbm, sem):
-    copies = []
-    for i, (source, target) in enumerate([(gq, gq_hbm), (gk, gk_hbm), (gv, gv_hbm)]):
-        for h in range(source.shape[0]):
-            copies.append(pltpu.make_async_copy(
-                source.at[h], target.at[:, pl.ds(h * DH, DH)], sem.at[i, h]
-            ))
-    for copy in copies:
+def store(gq, gk, gv, key, sym, gq_hbm, gk_hbm, gv_hbm, total, sem):
+    heads = gk.shape[0]
+
+    def copies(i, source, target):
+        return [
+            pltpu.make_async_copy(source.at[h], target.at[:, pl.ds(h * DH, DH)], sem.at[i, h])
+            for h in range(heads)
+        ]
+
+    early = copies(0, gq, gq_hbm) + copies(1, gv, gv_hbm)
+    late = copies(2, total, gk_hbm)
+    for copy in early:
         copy.start()
-    for copy in copies:
+    for h in range(heads):
+        k = key[h]
+        total[h] = gk[h] + nn(beside(k, k), sym[h])
+        late[h].start()
+    for copy in early + late:
         copy.wait()
 
 
@@ -463,7 +532,7 @@
     n_seq, n_head = lax.axis_size("seq"), lax.axis_size("head")
     span = n_seq // 4
     slots = max(span - 1, 1)
-    copies = 7 + (6 if span == 2 else 3 * (span - 1))
+    copies = 15 + (6 if span == 2 else 3 * (span - 1))
     vmem = pl.BlockSpec(memory_space=pltpu.VMEM)
     hbm = pl.BlockSpec(memory_space=pltpu.HBM)
     flat = jax.ShapeDtypeStruct((tok, cols), F32)
@@ -477,15 +546,16 @@
     results = pl.pallas_call(
         functools.partial(mega, span, n_seq, n_head),
         name="layer",
-        out_shape=[kept, kept, kept],
+        out_shape=[kept, kept, kept, pltpu.VMEM((heads, tok, DH), BF), pltpu.VMEM((heads, 2 * DH, DH), BF)],
         in_specs=[hbm] * 6,
-        out_specs=[vmem, vmem, vmem],
+        out_specs=[vmem] * 5,
         scratch_shapes=[
             pltpu.SMEM((heads,), F32), rows_bf, rows_bf, pltpu.VMEM((n_head,) + d_layer.shape, BF),
             pltpu.VMEM(out_weight.shape, BF), pltpu.VMEM((tok, cols), F32), rows_bf, rows_bf, turned_bf,
             mats_bf, mats_bf, pltpu.VMEM((slots, heads, DH, 2 * DH), BF), mat_bf, mat_bf, mat_bf, mat_bf,
             pltpu.VMEM((slots, heads, DH, DH), BF), pltpu.VMEM((slots, heads, DH, DH), BF),
             head_bf, head_bf, turned_bf, turned_bf, turned_bf,
+            rows_bf, rows_bf, head_bf, pltpu.VMEM((heads, DH, half), BF),
             pltpu.VMEM((2, heads, tok, 2 * DH), BF),
             pltpu.VMEM((2, heads, DH, tok), BF),
             pltpu.VMEM((2, heads, tok, DH), BF),
@@ -496,7 +566,7 @@
             pltpu.VMEM((2, heads, DH, 2 * DH), F32),
             pltpu.VMEM((2, heads, DH, 2 * DH), BF),
             pltpu.VMEM((2, heads, DH, 2 * DH), BF),
-            vec, vec, vec, vec,
+            vec, vec, pltpu.VMEM((heads, 2 * DH, half), BF), vec, vec,
             pltpu.VMEM((heads, 1, half), F32),
             pltpu.SemaphoreType.DMA((6,)),
             pltpu.SemaphoreType.DMA((2 * PIECES * n_head,)),
@@ -515,9 +585,9 @@
         store,
         name="store",
         out_shape=[flat, flat, flat],
-        in_specs=[vmem, vmem, vmem],
+        in_specs=[vmem] * 5,
         out_specs=[hbm, hbm, hbm],
-        scratch_shapes=[pltpu.SemaphoreType.DMA((3, heads))],
+        scratch_shapes=[pltpu.VMEM((heads, tok, DH), F32), pltpu.SemaphoreType.DMA((3, heads))],
         compiler_params=pltpu.CompilerParams(vmem_limit_bytes=8 * 1024 * 1024),
     )(*(pltpu.with_memory_space_constraint(result, pltpu.VMEM) for result in results))
 

time: 38.9 us -> 38.2 us (0.982); the launches traced: 38.1 us -> 38 us
  no operation moved by 1% of the time
where the time goes in v4:
time: 38.2 us; the launch traced here: 38 us
  Pallas kernels  37.4 us (98%)
  between operations  0.64 us (2%)
    pallas_call x1, Pallas kernels, body(): pl.pallas_call(functools.partial(mega, span, n_seq, n_head), name='layer'...  36.1 us
    pallas_call x1, Pallas kernels, body(): pl.pallas_call(store, name='store', out_shape=[flat, flat, flat], in_spec...  1.26 us

profile of v4, /device:TPU:0, one launch (start us, length us, event | category | flops | bytes accessed | tf_op | source)
XLA Modules:
  0.0 38.0 jit_solution(3045719149180745815)
XLA Ops:
  0.6 36.1 %layer.1 = (f32[4,256,128]{2,1,0:T(8,128)S(1)}, f32[4,256,128]{2,1,0:T(8,128)S(1)}, f32[4,256,128]{2,1,0:T(8,128)S(1)}, bf16[4,256,128]{2,1,0:T(8,128)(2,1)S(1)}, bf16[4,256,128]{2,1,0:T(8,128)(2,1)S(1)}) custom-call(f32[4]{0:T(128)} %ridge_hbm.1, bf16[256,512]{1,0:T(8,128)(2,1)} %key_hbm.1, bf16[256,512]{1,0:T(8,128)(2,1)} %val_hbm.1, ...), custom_call_target="tpu_custom_call" | custom-call | tf_op jit(solution)/shard_map/layer/pallas_call | solution.py:546
  36.7 1.3 %store.1 = (f32[256,512]{1,0:T(8,128)}, f32[256,512]{1,0:T(8,128)}, f32[256,512]{1,0:T(8,128)}) custom-call(f32[4,256,128]{2,1,0:T(8,128)S(1)} %get-tuple-element.8.gq, f32[4,256,128]{2,1,0:T(8,128)S(1)} %get-tuple-element.9.gk, f32[4,256,128]{2,1,0:T(8,128)S(1)} %get-tuple-element.10.gv, bf16[4,256,128]{2,1,0:T(8,128)(2,1)S(1)} %get-tuple-element.11.key, ...), custom_call_target="tpu_custom_call" | custom-call | tf_op jit(solution)/shard_map/store/pallas_call | solution.py:584

commit v5 on v4

--- a/solution.py
+++ b/solution.py
@@ -62,7 +62,7 @@
 def mega(span, n_seq, n_head, ridge_hbm, key_hbm, val_hbm, d_hbm, w_hbm, sav_hbm, gq, gk, gv, key_out, sym_out,
          ridge, key, val, d_all, w, sav, key_lag, val_lag, ot_s,
          mid, mid_lag, mid_in, cross, sym, cross_lead, sym_lead, cross_in, sym_in,
-         x_bf, x_lead, o_lead, y_bf, y_lead, key_stop, val_stop, x_stop, o_stop,
+         x_bf, x_lead, o_lead, y_bf, y_lead, key_stop, val_stop, x_stop, o_stop, sym_first,
          k2_s, kt_s, vc_s, xs_s, xt_s, a1_s, vs_s, full_s, g_s, st_s, r_s, p_s, p2_s, ya_s, yb_s, rr_s,
          local_sem, dsend_sem, drecv_sem, send_sem, recv_sem):
     s = lax.axis_index("seq")
@@ -360,9 +360,9 @@
         if between is None:
             lax.fori_loop(0, ITERS - 1, step, 0)
         else:
-            lax.fori_loop(0, ITERS // 2, step, 0)
+            lax.fori_loop(0, 1, step, 0)
             between()
-            lax.fori_loop(ITERS // 2, ITERS - 1, step, 0)
+            lax.fori_loop(1, ITERS - 1, step, 0)
         found = curves()
         for h in range(heads):
             y = y_s[c][h] + rr_s[h] / found[h][2] * p_s[h]
@@ -393,11 +393,11 @@
     def halfway():
         for k, q in rest[len(rest) // 2 :]:
             d_relay(k, q)
-        o_hops[0].forward()
 
     begin(0)
     iterate(0, halfway)
     y_hops = [Hop(y_bf.at[0], y_lead.at[0], -span).start()]
+    o_hops[0].forward()
     project(1)
     o_hops.append(Hop(ot_s.at[1], o_lead.at[1], -span).start())
     begin(1)
@@ -471,7 +471,9 @@
     y_hops[0].arrive()
     pairs = [nt(flipped[0][h], y_lead[0, h]) for h in every]
     for h in every:
-        to_k, to_v = apply_states(crosses[0][h], negative_sym(pairs[h]), k2_s[1, h, :half, :DH], vc_s[1, h, :half])
+        state = negative_sym(pairs[h])
+        sym_first[h] = state
+        to_k, to_v = apply_states(crosses[0][h], state, k2_s[1, h, :half, :DH], vc_s[1, h, :half])
         gk[h, rows[1]] = gk[h, rows[1]] + to_k
         gv[h, rows[1]] = gv[h, rows[1]] + to_v
     lead_part(0)
@@ -481,9 +483,9 @@
         apply_cross()
     y_hops[1].arrive()
     if paired:
-        lates = [nt(flipped[1][h], y_lead[1, h]) for h in every]
-        for h in every:
-            sym_lead[h] = negative_sym(pairs[h] + lates[h]).astype(BF)
+        lates = [nt(flipped[1][h], y_lead[1, h]) + nt(y_lead[1, h], flipped[1][h]) for h in every]
+        for h in every:
+            sym_lead[h] = (sym_first[h] - lates[h]).astype(BF)
         sym_hops.append(Hop(sym_lead, sym_in.at[0], 1, even, odd).start())
     lead_part(1)
     for hop in sym_hops:
@@ -555,7 +557,7 @@
             mats_bf, mats_bf, pltpu.VMEM((slots, heads, DH, 2 * DH), BF), mat_bf, mat_bf, mat_bf, mat_bf,
             pltpu.VMEM((slots, heads, DH, DH), BF), pltpu.VMEM((slots, heads, DH, DH), BF),
             head_bf, head_bf, turned_bf, turned_bf, turned_bf,
-            rows_bf, rows_bf, head_bf, pltpu.VMEM((heads, DH, half), BF),
+            rows_bf, rows_bf, head_bf, pltpu.VMEM((heads, DH, half), BF), pltpu.VMEM((heads, DH, DH), F32),
             pltpu.VMEM((2, heads, tok, 2 * DH), BF),
             pltpu.VMEM((2, heads, DH, tok), BF),
             pltpu.VMEM((2, heads, tok, DH), BF),

time: 38.2 us -> 38.1 us (level)
  no operation moved by 1% of the time
where the time goes in v5:
time: 38.1 us; the launch traced here: 38 us
  Pallas kernels  37.3 us (98%)
  between operations  0.64 us (2%)
    pallas_call x1, Pallas kernels, body(): pl.pallas_call(functools.partial(mega, span, n_seq, n_head), name='layer'...  36.1 us
    pallas_call x1, Pallas kernels, body(): pl.pallas_call(store, name='store', out_shape=[flat, flat, flat], in_spec...  1.26 us

profile of v5, /device:TPU:0, one launch (start us, length us, event | category | flops | bytes accessed | tf_op | source)
XLA Modules:
  0.0 38.0 jit_solution(6344663698215474043)
XLA Ops:
  0.6 36.1 %layer.1 = (f32[4,256,128]{2,1,0:T(8,128)S(1)}, f32[4,256,128]{2,1,0:T(8,128)S(1)}, f32[4,256,128]{2,1,0:T(8,128)S(1)}, bf16[4,256,128]{2,1,0:T(8,128)(2,1)S(1)}, bf16[4,256,128]{2,1,0:T(8,128)(2,1)S(1)}) custom-call(f32[4]{0:T(128)} %ridge_hbm.1, bf16[256,512]{1,0:T(8,128)(2,1)} %key_hbm.1, bf16[256,512]{1,0:T(8,128)(2,1)} %val_hbm.1, ...), custom_call_target="tpu_custom_call" | custom-call | tf_op jit(solution)/shard_map/layer/pallas_call | solution.py:548
  36.7 1.3 %store.1 = (f32[256,512]{1,0:T(8,128)}, f32[256,512]{1,0:T(8,128)}, f32[256,512]{1,0:T(8,128)}) custom-call(f32[4,256,128]{2,1,0:T(8,128)S(1)} %get-tuple-element.8.gq, f32[4,256,128]{2,1,0:T(8,128)S(1)} %get-tuple-element.9.gk, f32[4,256,128]{2,1,0:T(8,128)S(1)} %get-tuple-element.10.gv, bf16[4,256,128]{2,1,0:T(8,128)(2,1)S(1)} %get-tuple-element.11.key, ...), custom_call_target="tpu_custom_call" | custom-call | tf_op jit(solution)/shard_map/store/pallas_call | solution.py:586

commit v6 on v5

--- a/solution.py
+++ b/solution.py
@@ -137,8 +137,8 @@
                 def _():
                     target[...] = jnp.zeros(target.shape, target.dtype)
 
-        def start(self):
-            pl.when(self.sender)(self.copy.start)
+        def start(self, only=None):
+            pl.when(self.sender if only is None else jnp.logical_and(self.sender, only))(self.copy.start)
             return self
 
         def arrive(self):
@@ -184,9 +184,9 @@
             device_id_type=MESH,
         )
 
-    def d_start(q):
-        pl.when(has_right)(lambda: d_copy(me, q, 1).start())
-        pl.when(has_left)(lambda: d_copy(me, q, -1).start())
+    def d_start(q, only=True):
+        pl.when(jnp.logical_and(has_right, only))(lambda: d_copy(me, q, 1).start())
+        pl.when(jnp.logical_and(has_left, only))(lambda: d_copy(me, q, -1).start())
 
     def d_relay(k, q):
         @pl.when(jnp.logical_and(me - k >= 0, has_right))
@@ -262,9 +262,11 @@
             for q in pieces[0]:
                 d_relay(k, q)
         if late:
-            d_start(late.pop(0))
+            d_start(late.pop(0), even)
         if k == 1:
             key_hop.forward()
+    for q in pieces[1]:
+        d_start(q, odd)
     val_hop.forward()
     x_hop.forward()
     rest = [(k, q) for k in range(1, n_head - 1) for q in pieces[1]]
@@ -273,6 +275,8 @@
     rest = rest[2:]
     for h in range(heads):
         key_out[h] = key[:, cols(h)]
+    for c in range(2):
+        y_s[c][...] = jnp.zeros(y_s[c].shape, F32)
     w_copy.wait()
     ridge_copy.wait()
     project(0)
@@ -321,7 +325,6 @@
             r_s[h] = rs[h]
             p_s[h] = rs[h]
             p2_s[h] = above(*split(rs[h]))
-            y_s[c][h] = jnp.zeros_like(rs[h])
             rr_s[h] = jnp.sum(rs[h] * rs[h], axis=0, keepdims=True)
 
     def iterate(c, between=None):
@@ -358,7 +361,7 @@
             return carry
 
         if between is None:
-            lax.fori_loop(0, ITERS - 1, step, 0)
+            lax.fori_loop(0, ITERS - 1, step, 0, unroll=True)
         else:
             lax.fori_loop(0, 1, step, 0)
             between()
@@ -402,7 +405,7 @@
     o_hops.append(Hop(ot_s.at[1], o_lead.at[1], -span).start())
     begin(1)
     iterate(1)
-    y_hops.append(Hop(y_bf.at[1], y_lead.at[1], -span).start())
+    y_hops.append(Hop(y_bf.at[1], y_lead.at[1], -span).start(even if paired else None))
 
     crosses = [[nt(xt_s[c, h], twice(ot_s[c, h])) for h in every] for c in range(2)]
     pairs = [[], []]
@@ -414,6 +417,7 @@
         cross[h] = (crosses[0][h] + crosses[1][h]).astype(BF)
         sym[h] = negative_sym(pairs[0][h] + pairs[1][h]).astype(BF)
     if paired:
+        y_hops[1].start(odd)
         cross_hops = [Hop(cross, cross_in.at[0], -1, odd, even).start()]
         sym_hops = [Hop(sym, sym_in.at[0], -1, odd, even).start()]
     else:
@@ -481,6 +485,19 @@
         hop.arrive()
     if span > 1:
         apply_cross()
+    for j in range(n_head):
+        @pl.when(jnp.logical_and(has_right, j <= me))
+        def _():
+            for q in range(PIECES):
+                d_copy(j, q, 1).wait_send()
+
+        @pl.when(jnp.logical_and(has_left, j >= me))
+        def _():
+            for q in range(PIECES):
+                d_copy(j, q, -1).wait_send()
+    finished = [hop for hop in hops if hop is not y_hops[1]]
+    for hop in finished:
+        hop.finish()
     y_hops[1].arrive()
     if paired:
         lates = [nt(flipped[1][h], y_lead[1, h]) + nt(y_lead[1, h], flipped[1][h]) for h in every]
@@ -492,18 +509,9 @@
         hop.arrive()
     for h in every:
         sym_out[h] = above(*split(slots_sum(sym_in, h))) if span > 1 else jnp.zeros(sym_out.shape[1:], BF)
-    for j in range(n_head):
-        @pl.when(jnp.logical_and(has_right, j <= me))
-        def _():
-            for q in range(PIECES):
-                d_copy(j, q, 1).wait_send()
-
-        @pl.when(jnp.logical_and(has_left, j >= me))
-        def _():
-            for q in range(PIECES):
-                d_copy(j, q, -1).wait_send()
     for hop in hops:
-        hop.finish()
+        if hop not in finished:
+            hop.finish()
 
 
 def store(gq, gk, gv, key, sym, gq_hbm, gk_hbm, gv_hbm, total, sem):

time: 38.1 us -> 38.2 us (level)
  no operation moved by 1% of the time
where the time goes in v6:
time: 38.2 us; the launch traced here: 38.1 us
  Pallas kernels  37.3 us (98%)
  between operations  0.8 us (2%)
    pallas_call x1, Pallas kernels, body(): pl.pallas_call(functools.partial(mega, span, n_seq, n_head), name='layer'...  36 us
    pallas_call x1, Pallas kernels, body(): pl.pallas_call(store, name='store', out_shape=[flat, flat, flat], in_spec...  1.26 us

profile of v6, /device:TPU:0, one launch (start us, length us, event | category | flops | bytes accessed | tf_op | source)
XLA Modules:
  0.0 38.1 jit_solution(16986249147066057187)
XLA Ops:
  0.6 36.0 %layer.1 = (f32[4,256,128]{2,1,0:T(8,128)S(1)}, f32[4,256,128]{2,1,0:T(8,128)S(1)}, f32[4,256,128]{2,1,0:T(8,128)S(1)}, bf16[4,256,128]{2,1,0:T(8,128)(2,1)S(1)}, bf16[4,256,128]{2,1,0:T(8,128)(2,1)S(1)}) custom-call(f32[4]{0:T(128)} %ridge_hbm.1, bf16[256,512]{1,0:T(8,128)(2,1)} %key_hbm.1, bf16[256,512]{1,0:T(8,128)(2,1)} %val_hbm.1, ...), custom_call_target="tpu_custom_call" | custom-call | tf_op jit(solution)/shard_map/layer/pallas_call | solution.py:556
  36.7 1.3 %store.1 = (f32[256,512]{1,0:T(8,128)}, f32[256,512]{1,0:T(8,128)}, f32[256,512]{1,0:T(8,128)}) custom-call(f32[4,256,128]{2,1,0:T(8,128)S(1)} %get-tuple-element.8.gq, f32[4,256,128]{2,1,0:T(8,128)S(1)} %get-tuple-element.9.gk, f32[4,256,128]{2,1,0:T(8,128)S(1)} %get-tuple-element.10.gv, bf16[4,256,128]{2,1,0:T(8,128)(2,1)S(1)} %get-tuple-element.11.key, ...), custom_call_target="tpu_custom_call" | custom-call | tf_op jit(solution)/shard_map/store/pallas_call | solution.py:594
